TPU v7x, 128 devices: a whole 4x4x4 slice. The times are simulated.
128 devices in a mesh: expert: 8 (over z_lo, x), shard: 16 (over z_hi, y, core).
Axes of the slice: x: 4, y: 4, z: 4 (z_hi: 2, z_lo: 2; z = z_hi * 2 + z_lo), core: 2. Of those that a mesh axis runs over, the one named last changes fastest.
Arguments:
- master_gate: float32 [128, 2048, 768], P('expert', 'shard'), may hold values from -0.1875 to 0.1875
- second_gate: bfloat16 [128, 2048, 768], P('expert', 'shard'), may hold values from -0.0625 to 0.0625
- master_up: float32 [128, 2048, 768], P('expert', 'shard'), may hold values from -0.1875 to 0.1875
- second_up: bfloat16 [128, 2048, 768], P('expert', 'shard'), may hold values from -0.0625 to 0.0625
- router_weight: float32 [2048, 128], P('shard', 'expert'), may hold values from -0.125 to 0.125
- router_gain: float32 [2048], P('shard'), may hold values from 0.25 to 1.75
Outputs:
- final_gate: bfloat16 [128, 2048, 768], P(('expert', 'shard'))
- final_up: bfloat16 [128, 2048, 768], P(('expert', 'shard'))
- scale_gate: float32 [128, 768], P(('expert', 'shard'))
- scale_up: float32 [128, 768], P(('expert', 'shard'))
- serve_router: bfloat16 [2048, 128], replicated
All inputs are finite; a program needn't handle non-finite values. Where the computation divides by a largest or mean magnitude, that divisor is 1e-20 or more.
Results may differ from a plain program's by a relative error of at most 0.0085.
Values may be sent and summed in bfloat16 or wider, within the bound.
No kernel may reach another device: no remote copies, remote signals or barrier semaphores. Data moves between devices by JAX's collectives and lax.ppermute only.
A program may use at most 128 MiB of HBM per device.

v0:
```python
import jax
import jax.numpy as jnp
from jax import lax
from jax.sharding import Mesh
from jax.sharding import PartitionSpec as P

D_MODEL = 2048
EXPERT = ("expert_0", "expert_1")
EXPERT_SHARD = ("expert_0", "expert_1", "shard")


def side_by_side(arrays, axis, split_dim, concat_dim, along):
    both = jnp.concatenate(arrays, axis=along)
    out, at, finished = (
        lax.all_to_all(both, axis, split_axis=split_dim, concat_axis=concat_dim, tiled=True),
        0,
        [],
    )
    for a in arrays:
        finished.append(lax.slice_in_dim(out, at, at + a.shape[along], axis=along))
        at += a.shape[along]
    return tuple(finished)


def sent_to_all(array, axis):
    size = lax.axis_size(axis)
    return lax.all_to_all(
        jnp.broadcast_to(array[None], (size, *array.shape)), axis, 0, 0, tiled=True
    )


def laid_out(tiles, dim):
    shape = list(tiles.shape[1:])
    shape[dim] *= tiles.shape[0]
    return jnp.moveaxis(tiles, 0, dim).reshape(shape)


def gathered_copies(array, axis, dim):
    tiles = sent_to_all(array, axis)
    return laid_out(tiles, dim)


def all_blocks(array, axes, order):
    tiles = array[None]
    for k in order:
        tiles = lax.all_gather(tiles, axes[k], axis=0, tiled=True)
    current = [lax.axis_size(axes[k]) for k in reversed(order)]
    tiles = tiles.reshape(*current, *array.shape)
    turned = sorted(range(len(order)), key=lambda place: order[len(order) - 1 - place])
    return tiles.transpose(*turned, *range(len(order), tiles.ndim)).reshape(-1, *array.shape)


def gather_axes(array, axes, order, dim):
    return laid_out(all_blocks(array, axes, order), dim)


def shards(master_gate, second_gate, master_up, second_up, router_weight, router_gain):
    merged_gate = master_gate + second_gate.astype(jnp.float32)
    merged_up = master_up + second_up.astype(jnp.float32)
    whole_gate, whole_up = tuple(
        (
            part.astype(jnp.float32)
            for part in side_by_side(
                (merged_gate.astype(jnp.bfloat16), merged_up.astype(jnp.bfloat16)), "shard", 0, 1, 2
            )
        )
    )
    scale_gate = jnp.sum(jnp.abs(whole_gate), axis=1) / D_MODEL
    final_gate = (whole_gate / jnp.expand_dims(scale_gate, 1)).astype(jnp.bfloat16)
    scale_up = jnp.sum(jnp.abs(whole_up), axis=1) / D_MODEL
    final_up = (whole_up / jnp.expand_dims(scale_up, 1)).astype(jnp.bfloat16)
    part_router = (router_weight * router_gain[:, None]).astype(jnp.bfloat16)
    row_router = gathered_copies(part_router, "shard", 0)
    serve_router = gather_axes(row_router, EXPERT, (0, 1), 1)
    return (final_gate, final_up, scale_gate, scale_up, serve_router)


def solution(mesh):
    split = Mesh(mesh.devices.reshape(2, 4, mesh.shape["shard"]), ("expert_0", "expert_1", "shard"))
    return jax.shard_map(
        shards,
        mesh=split,
        in_specs=(
            P(EXPERT, "shard", None),
            P(EXPERT, "shard", None),
            P(EXPERT, "shard", None),
            P(EXPERT, "shard", None),
            P("shard", EXPERT),
            P("shard"),
        ),
        out_specs=(
            P(EXPERT_SHARD, None, None),
            P(EXPERT_SHARD, None, None),
            P(EXPERT_SHARD, None),
            P(EXPERT_SHARD, None),
            P(),
        ),
        check_vma=False,
    )
```

profile of v0, /device:TPU:10, one launch (start us, length us, event | category | flops | bytes accessed | tf_op | source)
XLA Modules:
  0.0 128.7 jit_solution(17627529995646358045)
XLA Ops:
  0.6 0.7 multiply_convert_fusion
  1.3 0.6 broadcast_in_dim.2
  2.0 8.2 %all-to-all-start.1 = ((bf16[16,128,16]{1,2,0:T(8,128)(2,1)}), bf16[16,128,16]{1,2,0:T(8,128)(2,1)S(1)}, u32[]{:S(2)}, u32[]{:S(2)}) async-start(bf16[16,128,16]{1,2,0:T(8,128)(2,1)} %broadcast_in_dim.2), calls=%async_computation.1 | async-start | bytes 131072 | tf_op jit(solution)/shard_map/all_to_all | solution.py:27
  10.2 10.1 %add_convert_fusion = (bf16[16,128,768]{2,1,0:T(8,128)(2,1)S(1)}, bf16[16,128,768]{2,1,0:T(8,128)(2,1)}) fusion(f32[16,128,768]{2,1,0:T(8,128)} %param.8, bf16[16,128,768]{2,1,0:T(8,128)(2,1)} %param.9, f32[16,128,768]{2,1,0:T(8,128)} %param.6, bf16[16,128,768]{2,1,0:T(8,128)(2,1)} %param.7), kind=kLoop, calls=%fused_computation.9 | loop fusion | flops 9437184 | bytes 25165824 | tf_op jit(solution)/shard_map/convert_element_type | solution.py:64
  20.4 5.1 %pad_maximum_fusion = bf16[16,128,1536]{2,1,0:T(8,128)(2,1)} fusion(bf16[16,128,768]{2,1,0:T(8,128)(2,1)S(1)} %get-tuple-element.29, bf16[16,128,768]{2,1,0:T(8,128)(2,1)} %get-tuple-element.30), kind=kLoop, calls=%fused_computation.8 | loop fusion | flops 12582912 | bytes 12582912 | tf_op jit(solution)/shard_map/concatenate | solution.py:13
  25.5 0.0 all-to-all-done.1
  25.5 7.2 %all-to-all-start = ((bf16[16,128,1536]{2,1,0:T(8,128)(2,1)}), bf16[16,128,1536]{2,1,0:T(8,128)(2,1)}, u32[]{:S(2)}, u32[]{:S(2)}) async-start(bf16[16,128,1536]{2,1,0:T(8,128)(2,1)} %pad_maximum_fusion), calls=%async_computation | async-start | bytes 12582912 | tf_op jit(solution)/shard_map/all_to_all | solution.py:15
  32.7 70.9 %all_gather.6 = bf16[2,2048,16]{1,2,0:T(8,128)(2,1)S(1)} all-gather(bf16[1,2048,16]{1,2,0:T(8,128)(2,1)S(1)} %broadcast_in_dim_reshape.3), channel_id=1, replica_groups=mesh['expert_0'=2,'expert_1'=4,'shard'=16] {'expert_0'}, dimensions={0}, use_global_device_ids=true | all-gather | bytes 196608 | tf_op jit(solution)/shard_map/all_gather | solution.py:46
  103.7 13.5 %all_gather.7 = bf16[8,2048,16]{1,2,0:T(8,128)(2,1)S(1)} all-gather(bf16[2,2048,16]{1,2,0:T(8,128)(2,1)S(1)} %all_gather.6), channel_id=1, replica_groups=mesh['expert_0'=2,'expert_1'=4,'shard'=16] {'expert_1'}, dimensions={0}, use_global_device_ids=true | all-gather | bytes 655360 | tf_op jit(solution)/shard_map/all_gather | solution.py:46
  117.2 1.0 copy.19
  118.2 0.0 all-to-all-done
  118.2 4.1 %fusion.2 = (f32[768]{0:T(1024)S(1)}, f32[768]{0:T(1024)S(1)}) fusion(bf16[1,2048,1536]{2,1,0:T(8,128)(2,1)} %bitcast), kind=kLoop, calls=%fused_computation.6 | loop fusion | flops 9435648 | bytes 6297600 | tf_op jit(solution)/shard_map/reduce_sum | solution.py:70
  122.4 0.6 div.32
  122.9 5.2 %fusion.3 = (bf16[1,2048,768]{2,1,0:T(8,128)(2,1)}, bf16[1,2048,768]{2,1,0:T(8,128)(2,1)}) fusion(f32[768]{0:T(1024)S(1)} %broadcast_multiply_fusion, bf16[1,2048,1536]{2,1,0:T(8,128)(2,1)} %bitcast, f32[768]{0:T(1024)S(1)} %broadcast_multiply_fusion.1), kind=kLoop, calls=%fused_computation.7 | loop fusion | flops 9437184 | bytes 12589056 | tf_op jit(solution)/shard_map/convert_element_type | solution.py:71
  128.2 0.6 div.33
  (5 shorter events, 0.1 us)
Async XLA Ops:
  2.0 23.5 %all-to-all-start.1 = ((bf16[16,128,16]{1,2,0:T(8,128)(2,1)}), bf16[16,128,16]{1,2,0:T(8,128)(2,1)S(1)}, u32[]{:S(2)}, u32[]{:S(2)}) async-start(bf16[16,128,16]{1,2,0:T(8,128)(2,1)} %broadcast_in_dim.2), calls=%async_computation.1 | async-start | bytes 131072 | tf_op jit(solution)/shard_map/all_to_all | solution.py:27
  25.5 92.8 %all-to-all-start = ((bf16[16,128,1536]{2,1,0:T(8,128)(2,1)}), bf16[16,128,1536]{2,1,0:T(8,128)(2,1)}, u32[]{:S(2)}, u32[]{:S(2)}) async-start(bf16[16,128,1536]{2,1,0:T(8,128)(2,1)} %pad_maximum_fusion), calls=%async_computation | async-start | bytes 12582912 | tf_op jit(solution)/shard_map/all_to_all | solution.py:15
where the time goes:
time: 129 us
  blocking collectives  84.4 us (65%)
  other arithmetic  25.3 us (20%)
  starting transfers between devices  15.5 us (12%)
  local copies, waits for them, and re-layouts  2.89 us (2%)
    all_gather x2, blocking collectives, all_blocks(): tiles = lax.all_gather(tiles, axes[k], axis=0, tiled=True)  84.4 us
    convert_element_type x1, other arithmetic, shards(): merged_up.astype(jnp.bfloat16)  10.1 us
    all_to_all x1, starting transfers between devices, sent_to_all(): lax.all_to_all(jnp.broadcast_to(array[None], (size, *array.shape)), axis,...  8.24 us
    all_to_all x1, starting transfers between devices, side_by_side(): lax.all_to_all(both, axis, split_axis=split_dim, concat_axis=concat_dim,...  7.23 us
    convert_element_type x1, other arithmetic, shards(): final_up = (whole_up / jnp.expand_dims(scale_up, 1)).astype(jnp.bfloat16)  5.21 us
    concatenate x1, other arithmetic, side_by_side(): both = jnp.concatenate(arrays, axis=along)  5.1 us
    reduce_sum x1, other arithmetic, shards(): scale_up = jnp.sum(jnp.abs(whole_up), axis=1) / D_MODEL  4.12 us
  transfers between devices with their start and end apart: 2, of which 0 were waited for; matrix products, arithmetic and copies ran while one was open for 13% of the time, Pallas kernels for 0%

commit v1 on v0

v1 whole, which is shorter than its diff:
```python
from itertools import product

import jax
import jax.numpy as jnp
from jax import lax
from jax.experimental import pallas as pl
from jax.experimental.pallas import tpu as pltpu
from jax.sharding import Mesh
from jax.sharding import PartitionSpec as P


D_MODEL = 2048
LANES = 128
EXPERT = ("zl", "x")
SHARD = ("zh", "y", "c")
GROUPS = ("zl", "zh", "y", "c")
ROUNDS = (
    ((1, 0, 0), (0, 2, 0)),
    ((1, 0, 1), (0, 2, 1)),
    ((1, 1, 0), (0, 3, 0)),
    ((1, 1, 1), (0, 3, 1)),
    ((1, 3, 0), (0, 1, 0)),
    ((1, 3, 1), (0, 1, 1)),
    ((1, 2, 0), (0, 0, 1)),
    ((1, 2, 1), (0, 0, 0)),
)
BATCHES = ((0,), (1, 2), (3, 4), (5, 6, 7))
FINALS = (
    (((0, 0), (0, 1), (1, 0), (1, 1), (2, 0), (2, 1), (3, 0), (3, 1), (7, 1)), False),
    (((4, 0), (4, 1), (5, 0), (5, 1)), True),
    (((6, 0), (6, 1)), True),
    (((7, 0),), True),
)
DEPTH = 3
ANY = pl.BlockSpec(memory_space=pltpu.HBM)
VMEM = pl.BlockSpec(memory_space=pltpu.VMEM)


def ring(step):
    return [(z * 8 + y * 2 + c, (z + step[0]) % 2 * 8 + (y + step[1]) % 4 * 2 + (c + step[2]) % 2) for z, y, c in product(range(2), range(4), range(2))]


def place(step, sign):
    dz, dy, dc = step
    z, y, c = (lax.axis_index(a) for a in SHARD)
    dy = dy if sign > 0 else (4 - dy) % 4
    return lax.rem(z + dz, 2) * 8 + lax.rem(y + dy, 4) * 2 + lax.rem(c + dc, 2)


def in_hbm(x):
    return pltpu.with_memory_space_constraint(x, pltpu.HBM)


def params(mib):
    return pltpu.CompilerParams(vmem_limit_bytes=mib << 20)


def merge_chunks(steps, arrays, earlier=None, router=None):
    _, rows, cols = arrays[0].shape
    n = len(steps)
    last = earlier is not None
    old = [s for _, s in earlier] + list(router) if last else []
    wide = 2 * cols // LANES
    ranks = 16

    def body(*refs):
        ins, refs = refs[:4], refs[4:]
        olds, refs = refs[: len(old)], refs[len(old) :]
        outs, sums, refs = refs[:n], refs[n], refs[n + 1 :]
        bufs, obuf, isem, osem, pay = refs[:4], refs[4], refs[5], refs[6], refs[7]
        copies = []
        for k, s in enumerate(steps):
            e = place(s, 1)
            copies.append([pltpu.make_async_copy(a.at[e], b.at[k], isem.at[k, i]) for i, (a, b) in enumerate(zip(ins, bufs))])
            for c in copies[-1]:
                c.start()
        if last:
            part = (olds[-2][...] * olds[-1][...]).astype(jnp.bfloat16)
            for e in range(sums.shape[0]):
                sums[e, : part.shape[0], :] = part
            for (before, _), o in zip(earlier, olds):
                for k, s in enumerate(before):
                    pay[place(s, 1), :wide, :] = o[k]
        sent = []
        for k, o in enumerate(outs):
            for h in range(2):
                for c in copies[k][2 * h : 2 * h + 2]:
                    c.wait()
                m = bufs[2 * h][k] + bufs[2 * h + 1][k].astype(jnp.float32)
                obuf[k, :, h * cols : (h + 1) * cols] = m.astype(jnp.bfloat16)
                t = jnp.abs(m).reshape(rows // 8, 8, cols).sum(0).sum(0, keepdims=True)
                for j in range(cols // LANES):
                    at = h * (cols // LANES) + j
                    if last:
                        pay[place(steps[k], 1), at : at + 1, :] = t[:, j * LANES : (j + 1) * LANES]
                    else:
                        sums[k, at : at + 1, :] = t[:, j * LANES : (j + 1) * LANES]
            sent.append(pltpu.make_async_copy(obuf.at[k], o, osem.at[k]))
            sent[-1].start()
        if last:
            r = part.shape[0]
            tail = pay[...].astype(jnp.bfloat16)
            for z in range(sums.shape[0] // ranks):
                sums[z * ranks : (z + 1) * ranks, r:, :] = tail
        for c in sent:
            c.wait()

    size = n * rows * cols * 16
    if last:
        r = router[0].shape[0]
        extra = jax.ShapeDtypeStruct((lax.axis_size(GROUPS), 2 * r, LANES), jnp.bfloat16)
        pay = pltpu.VMEM((ranks, r, LANES), jnp.float32)
    else:
        extra = jax.ShapeDtypeStruct((n, wide, LANES), jnp.float32)
        pay = pltpu.VMEM((8, LANES), jnp.float32)
    return pl.pallas_call(
        body,
        in_specs=[ANY] * 4 + [VMEM] * len(old),
        out_specs=[ANY] * n + [VMEM],
        out_shape=[pltpu.HBM((rows, 2 * cols), jnp.bfloat16)] * n + [extra],
        scratch_shapes=[pltpu.VMEM((n, rows, cols), a.dtype) for a in arrays]
        + [pltpu.VMEM((n, rows, 2 * cols), jnp.bfloat16), pltpu.SemaphoreType.DMA((n, 4)), pltpu.SemaphoreType.DMA((n,)), pay],
        compiler_params=params((size >> 20) + 3),
        name="merge",
    )(*[in_hbm(a) for a in arrays], *old)


def finish(steps, chunks, got, before=None, near=False):
    rows, cols = chunks[0].shape
    n, half = len(steps), cols // 2
    wide = cols // LANES
    ranks = 16
    first = before is None
    kept = [] if first else list(before)

    def body(*refs):
        ins, got_ref, refs = refs[:n], refs[n], refs[n + 1 + len(kept) :]
        outs, refs = refs[:2], refs[2:]
        scales, refs = (refs[:2], refs[2:]) if first else (None, refs)
        obuf, osem, *refs = refs
        if not near:
            buf, isem = refs
            copies = [pltpu.make_async_copy(r, buf.at[k], isem.at[k]) for k, r in enumerate(ins)]
            for c in copies:
                c.start()
        mine = got_ref[pl.ds(pl.multiple_of(lax.axis_index("zl") * ranks, ranks), ranks), got_ref.shape[1] // 2 :, :]
        s = mine.astype(jnp.float32).sum(0)[:wide] * (1.0 / D_MODEL)
        if first:
            for j in range(wide):
                a, at = divmod(j * LANES, half)
                scales[a][:, at : at + LANES] = s[j : j + 1, :]
        inv = 1.0 / s
        sent = []
        for k in range(n):
            if not near:
                copies[k].wait()
            to = pl.ds(pl.multiple_of(place(steps[k], -1) * rows, rows), rows)
            for a in range(2):
                for j in range(a * wide // 2, (a + 1) * wide // 2):
                    at = slice(j * LANES, (j + 1) * LANES)
                    x = ins[k][:, at] if near else buf[k, :, at]
                    obuf[k, a, :, j * LANES - a * half : (j + 1) * LANES - a * half] = (x.astype(jnp.float32) * inv[j : j + 1, :]).astype(jnp.bfloat16)
                sent.append(pltpu.make_async_copy(obuf.at[k, a], outs[a].at[to], osem.at[k, a]))
                sent[-1].start()
        for c in sent:
            c.wait()

    full = pltpu.HBM((16 * rows, half), jnp.bfloat16)
    space = pltpu.VMEM if near else pltpu.HBM
    return pl.pallas_call(
        body,
        in_specs=[pl.BlockSpec(memory_space=space)] * n + [VMEM] + [ANY] * len(kept),
        out_specs=[ANY] * 2 + ([VMEM] * 2 if first else []),
        out_shape=[full] * 2 + ([jax.ShapeDtypeStruct((1, half), jnp.float32)] * 2 if first else []),
        scratch_shapes=[pltpu.VMEM((n, 2, rows, half), jnp.bfloat16), pltpu.SemaphoreType.DMA((n, 2))]
        + ([] if near else [pltpu.VMEM((n, rows, cols), jnp.bfloat16), pltpu.SemaphoreType.DMA((n,))]),
        input_output_aliases={} if first else {n + 1: 0, n + 2: 1},
        compiler_params=params(n + 3),
        name="finish",
    )(*[pltpu.with_memory_space_constraint(c, space) for c in chunks], got, *kept)


def lay_router(groups):
    _, s, e, rows = groups[0].shape
    e //= 2
    m = len(groups)

    def body(*refs):
        o_ref, buf = refs[m:]
        x = lax.axis_index("x")
        for k in range(s):
            for d in range(m):
                for w in range(2):
                    at = (w * m + lax.rem(x + m - d, m)) * e
                    buf[k, pl.ds(pl.multiple_of(at, e), e), :] = refs[d][w, k, :e, :].astype(jnp.float32)
            o_ref[k * rows : (k + 1) * rows, :] = buf[k].T.astype(jnp.bfloat16)

    return pl.pallas_call(
        body,
        out_shape=jax.ShapeDtypeStruct((s * rows, 2 * m * e), jnp.bfloat16),
        scratch_shapes=[pltpu.VMEM((s, 2 * m * e, rows), jnp.float32)],
        compiler_params=params(8),
        name="lay_router",
    )(*groups)


def exchange(x, axes):
    return lax.all_to_all(x, axes, 0, 0, tiled=True)


def tied(values, after):
    out = lax.optimization_barrier((*values, *after))
    return list(out[: len(values)]), list(out[len(values) :])


def shards(master_gate, second_gate, master_up, second_up, router_weight, router_gain):
    arrays = [master_gate, second_gate, master_up, second_up]
    chunks, sums = [], []
    for b, batch in enumerate(BATCHES):
        steps = [s for r in batch for s in ROUNDS[r]]
        last = b == len(BATCHES) - 1
        *made, part_sums = merge_chunks(steps, arrays, *((sums, (router_weight.T, router_gain[None])) if last else ()))
        sums.append((steps, part_sums))
        if not last:
            arrays, (made[0],) = tied(arrays, [made[0]])
        for r in batch:
            chunks.append(made[: len(ROUNDS[r])])
            made = made[len(ROUNDS[r]) :]
    small = exchange(sums[-1][1], GROUPS)
    cols = small.reshape(2, 16, *small.shape[1:])
    m = lax.axis_size("x")
    groups = [cols]
    for d in range(1, m):
        groups.append(lax.ppermute(cols, "x", [(i, (i + d) % m) for i in range(m)]))
    router = lay_router(groups)
    got = []
    for r, steps in enumerate(ROUNDS):
        vals = list(chunks[r])
        if r >= DEPTH:
            vals, got[r - DEPTH] = tied(vals, got[r - DEPTH])
        moved = []
        for v, s in zip(vals, steps):
            moved.append(lax.ppermute(v, SHARD, ring(s)) if any(s) else v)
        got.append(moved)
    finals, scales = None, None
    for places, near in FINALS:
        out = finish([ROUNDS[r][i] for r, i in places], [got[r][i] for r, i in places], small, finals, near)
        if finals is None:
            scales = out[2:]
        finals = out[:2]
    return finals[0][None], finals[1][None], *scales, router


def solution(mesh):
    split = Mesh(mesh.devices.reshape(2, 4, 2, 4, 2), ("zl", "x", "zh", "y", "c"))
    w = P(EXPERT, SHARD, None)
    out = P(EXPERT + SHARD, None, None)
    return jax.shard_map(
        shards,
        mesh=split,
        in_specs=(w, w, w, w, P(SHARD, EXPERT), P(SHARD)),
        out_specs=(out, out, P(EXPERT + SHARD, None), P(EXPERT + SHARD, None), P()),
        check_vma=False,
    )
```

time: 129 us -> 97 us (0.75)
  the two profiles are of different devices: /device:TPU:10 before, /device:TPU:1 now
where the time goes in v1:
time: 97 us; the launch traced here: 96.7 us
  starting transfers between devices  44.4 us (46%)
  waiting for transfers between devices  28.7 us (30%)
  Pallas kernels  22.8 us (24%)
    ppermute x15, starting transfers between devices, shards(): moved.append(lax.ppermute(v, SHARD, ring(s)) if any(s) else v)  34.3 us
    pallas_call x4, Pallas kernels, merge_chunks(): pl.pallas_call(body, in_specs=[ANY] * 4 + [VMEM] * len(old), out_specs=[A...  14.8 us
    all_to_all x1, waiting for transfers between devices, exchange(): return lax.all_to_all(x, axes, 0, 0, tiled=True)  13.1 us
    ppermute x15, waiting for transfers between devices, shards(): moved.append(lax.ppermute(v, SHARD, ring(s)) if any(s) else v)  12.4 us
    pallas_call x4, Pallas kernels, finish(): pl.pallas_call(body, in_specs=[pl.BlockSpec(memory_space=space)] * n + [V...  6.71 us
    all_to_all x1, starting transfers between devices, exchange(): return lax.all_to_all(x, axes, 0, 0, tiled=True)  5.28 us
    ppermute x3, starting transfers between devices, shards(): groups.append(lax.ppermute(cols, 'x', [(i, (i + d) % m) for i in range(m)]))  4.82 us
    ppermute x3, waiting for transfers between devices, shards(): groups.append(lax.ppermute(cols, 'x', [(i, (i + d) % m) for i in range(m)]))  3.18 us
  transfers between devices with their start and end apart: 19, of which 6 were waited for; matrix products, arithmetic and copies ran while one was open for 0% of the time, Pallas kernels for 20%

profile of v1, /device:TPU:1, one launch (start us, length us, event | category | flops | bytes accessed | tf_op | source)
XLA Modules:
  0.0 96.7 jit_solution(10451302716288798814)
XLA Ops:
  0.6 2.5 %merge.4 = (bf16[128,1536]{1,0:T(8,128)(2,1)}, bf16[128,1536]{1,0:T(8,128)(2,1)}, f32[2,12,128]{2,1,0:T(8,128)S(1)}) custom-call(f32[16,128,768]{2,1,0:T(8,128)} %refs_0_.4, bf16[16,128,768]{2,1,0:T(8,128)(2,1)} %refs_1_.4, f32[16,128,768]{2,1,0:T(8,128)} %refs_2_.4, bf16[16,128,768]{2,1,0:T(8,128)(2,1)} %refs_3_.4), custom_call_target="tpu_custom_call" | custom-call | tf_op jit(solution)/shard_map/merge/pallas_call | solution.py:116
  3.2 4.5 %collective-permute-start.5 = (bf16[128,1536]{1,0:T(8,128)(2,1)}, bf16[128,1536]{1,0:T(8,128)(2,1)S(1)}, u32[]{:S(2)}, u32[]{:S(2)}) collective-permute-start(bf16[128,1536]{1,0:T(8,128)(2,1)} %get-tuple-element.102), channel_id=1, source_target_pairs={{0,8},{1,9},{2,10},{3,11},{4,12},{5,13},{6,14},{7,15},{8,0},{9,1},... | collective-permute-start | bytes 1179656 | tf_op jit(solution)/shard_map/ppermute | solution.py:243
  7.7 2.9 %collective-permute-start.6 = (bf16[128,1536]{1,0:T(8,128)(2,1)}, bf16[128,1536]{1,0:T(8,128)(2,1)S(1)}, u32[]{:S(2)}, u32[]{:S(2)}) collective-permute-start(bf16[128,1536]{1,0:T(8,128)(2,1)} %get-tuple-element.103), channel_id=1, source_target_pairs={{0,4},{1,5},{2,6},{3,7},{4,0},{5,1},{6,2},{7,3},{8,12},{9,13},{10,... | collective-permute-start | bytes 1179656 | tf_op jit(solution)/shard_map/ppermute | solution.py:243
  10.6 3.5 %merge.5 = (bf16[128,1536]{1,0:T(8,128)(2,1)}, bf16[128,1536]{1,0:T(8,128)(2,1)}, bf16[128,1536]{1,0:T(8,128)(2,1)}, bf16[128,1536]{1,0:T(8,128)(2,1)}, f32[4,12,128]{2,1,0:T(8,128)S(1)}) custom-call(f32[16,128,768]{2,1,0:T(8,128)} %refs_0_.4, bf16[16,128,768]{2,1,0:T(8,128)(2,1)} %refs_1_.4, f32[16,128,768]{2,1,0:T(8,128)} %refs_2_.4, ...), custom_call_target="tpu_custom_call" | custom-call | tf_op jit(solution)/shard_map/merge/pallas_call | solution.py:116
  14.0 1.0 %collective-permute-start = (bf16[128,1536]{1,0:T(8,128)(2,1)}, bf16[128,1536]{1,0:T(8,128)(2,1)S(1)}, u32[]{:S(2)}, u32[]{:S(2)}) collective-permute-start(bf16[128,1536]{1,0:T(8,128)(2,1)} %get-tuple-element.92), channel_id=1, source_target_pairs={{0,9},{1,8},{2,11},{3,10},{4,13},{5,12},{6,15},{7,14},{8,1},{9,0},... | collective-permute-start | bytes 1179656 | tf_op jit(solution)/shard_map/ppermute | solution.py:243
  15.0 0.3 collective-permute-start.1
  15.4 3.0 %collective-permute-start.11 = (bf16[128,1536]{1,0:T(8,128)(2,1)}, bf16[128,1536]{1,0:T(8,128)(2,1)S(1)}, u32[]{:S(2)}, u32[]{:S(2)}) collective-permute-start(bf16[128,1536]{1,0:T(8,128)(2,1)} %get-tuple-element.112), channel_id=1, source_target_pairs={{0,10},{1,11},{2,12},{3,13},{4,14},{5,15},{6,8},{7,9},{8,2},{9,3},... | collective-permute-start | bytes 1179656 | tf_op jit(solution)/shard_map/ppermute | solution.py:243
  18.4 3.5 %merge.6 = (bf16[128,1536]{1,0:T(8,128)(2,1)}, bf16[128,1536]{1,0:T(8,128)(2,1)}, bf16[128,1536]{1,0:T(8,128)(2,1)}, bf16[128,1536]{1,0:T(8,128)(2,1)}, f32[4,12,128]{2,1,0:T(8,128)S(1)}) custom-call(f32[16,128,768]{2,1,0:T(8,128)} %refs_0_.4, bf16[16,128,768]{2,1,0:T(8,128)(2,1)} %refs_1_.4, f32[16,128,768]{2,1,0:T(8,128)} %refs_2_.4, ...), custom_call_target="tpu_custom_call" | custom-call | tf_op jit(solution)/shard_map/merge/pallas_call | solution.py:116
  21.9 0.0 collective-permute-done.5.refs_0_
  21.9 2.3 %collective-permute-start.12 = (bf16[128,1536]{1,0:T(8,128)(2,1)S(1)}, bf16[128,1536]{1,0:T(8,128)(2,1)S(1)}, u32[]{:S(2)}, u32[]{:S(2)}) collective-permute-start(bf16[128,1536]{1,0:T(8,128)(2,1)S(1)} %copy-done.10), channel_id=1, source_target_pairs={{0,6},{1,7},{2,0},{3,1},{4,2},{5,3},{6,4},{7,5},{8,14},{9,15},{10,... | collective-permute-start | bytes 1179656 | tf_op jit(solution)/shard_map/ppermute | solution.py:243
  24.2 0.0 collective-permute-done.6.refs_1_
  24.2 0.4 collective-permute-start.7
  24.7 2.4 %collective-permute-done.refs_2_ = bf16[128,1536]{1,0:T(8,128)(2,1)S(1)} collective-permute-done((bf16[128,1536]{1,0:T(8,128)(2,1)}, bf16[128,1536]{1,0:T(8,128)(2,1)S(1)}, u32[]{:S(2)}, u32[]{:S(2)}) %collective-permute-start) | collective-permute-done | bytes 393248 | tf_op jit(solution)/shard_map/ppermute | solution.py:243
  27.1 1.9 %collective-permute-start.8 = (bf16[128,1536]{1,0:T(8,128)(2,1)}, bf16[128,1536]{1,0:T(8,128)(2,1)}, u32[]{:S(2)}, u32[]{:S(2)}) collective-permute-start(bf16[128,1536]{1,0:T(8,128)(2,1)} %get-tuple-element.105), channel_id=1, source_target_pairs={{0,7},{1,6},{2,1},{3,0},{4,3},{5,2},{6,5},{7,4},{8,15},{9,14},{10,... | collective-permute-start | bytes 1179656 | tf_op jit(solution)/shard_map/ppermute | solution.py:243
  29.0 0.0 copy-done
  29.0 5.4 %merge.7 = (bf16[128,1536]{1,0:T(8,128)(2,1)}, bf16[128,1536]{1,0:T(8,128)(2,1)}, bf16[128,1536]{1,0:T(8,128)(2,1)}, bf16[128,1536]{1,0:T(8,128)(2,1)}, bf16[128...) custom-call(f32[16,128,768]{2,1,0:T(8,128)} %refs_0_.4, bf16[16,128,768]{2,1,0:T(8,128)(2,1)} %refs_1_.4, ...), custom_call_target="tpu_custom_call" | custom-call | tf_op jit(solution)/shard_map/merge/pallas_call | solution.py:116
  34.4 5.3 %all-to-all-start = ((bf16[32,32,128]{2,1,0:T(8,128)(2,1)}), bf16[32,32,128]{2,1,0:T(8,128)(2,1)S(1)}, u32[]{:S(2)}, u32[]{:S(2)}) async-start(bf16[32,32,128]{2,1,0:T(8,128)(2,1)} %get-tuple-element.97), calls=%async_computation | async-start | bytes 524288 | tf_op jit(solution)/shard_map/all_to_all | solution.py:208
  39.7 0.0 collective-permute-done.1.refs_3_
  39.7 5.0 %collective-permute-start.2 = (bf16[128,1536]{1,0:T(8,128)(2,1)S(1)}, bf16[128,1536]{1,0:T(8,128)(2,1)S(1)}, u32[]{:S(2)}, u32[]{:S(2)}) collective-permute-start(bf16[128,1536]{1,0:T(8,128)(2,1)S(1)} %copy-done.9), channel_id=1, source_target_pairs={{0,14},{1,15},{2,8},{3,9},{4,10},{5,11},{6,12},{7,13},{8,6},{9,7},... | collective-permute-start | bytes 1179656 | tf_op jit(solution)/shard_map/ppermute | solution.py:243
  44.8 0.0 collective-permute-done.11.refs_4_
  44.8 0.1 collective-permute-start.3
  44.9 13.1 %all-to-all-done.refs_9_.refs_4_.refs_2_.refs_1_ = bf16[32,32,128]{2,1,0:T(8,128)(2,1)S(1)} async-done(((bf16[32,32,128]{2,1,0:T(8,128)(2,1)}), bf16[32,32,128]{2,1,0:T(8,128)(2,1)S(1)}, u32[]{:S(2)}, u32[]{:S(2)}) %all-to-all-start) | async-done | bytes 262176 | tf_op jit(solution)/shard_map/all_to_all | solution.py:208
  58.0 0.0 collective-permute-done.12.refs_5_
  58.0 1.2 %collective-permute-start.15 = (bf16[2,16,32,128]{3,2,1,0:T(8,128)(2,1)S(1)}, bf16[2,16,32,128]{3,2,1,0:T(8,128)(2,1)S(1)}, u32[]{:S(2)}, u32[]{:S(2)}) collective-permute-start(bf16[2,16,32,128]{3,2,1,0:T(8,128)(2,1)S(1)} %bitcast.5), channel_id=1, source_target_pairs={{0,16},{16,32},{32,48},{48,0},{1,17},{17,33},{33,49},{49,1},{2,18}... | collective-permute-start | bytes 786440 | tf_op jit(solution)/shard_map/ppermute | solution.py:234
  59.2 0.0 collective-permute-done.7.refs_6_
  59.2 2.5 %collective-permute-start.16 = (bf16[2,16,32,128]{3,2,1,0:T(8,128)(2,1)S(1)}, bf16[2,16,32,128]{3,2,1,0:T(8,128)(2,1)S(1)}, u32[]{:S(2)}, u32[]{:S(2)}) collective-permute-start(bf16[2,16,32,128]{3,2,1,0:T(8,128)(2,1)S(1)} %bitcast.6), channel_id=1, source_target_pairs={{0,32},{16,48},{32,0},{48,16},{1,33},{17,49},{33,1},{49,17},{2,34}... | collective-permute-start | bytes 786440 | tf_op jit(solution)/shard_map/ppermute | solution.py:234
  61.6 0.0 collective-permute-done.8.refs_7_
  61.6 1.2 %collective-permute-start.17 = (bf16[2,16,32,128]{3,2,1,0:T(8,128)(2,1)S(1)}, bf16[2,16,32,128]{3,2,1,0:T(8,128)(2,1)S(1)}, u32[]{:S(2)}, u32[]{:S(2)}) collective-permute-start(bf16[2,16,32,128]{3,2,1,0:T(8,128)(2,1)S(1)} %bitcast.7), channel_id=1, source_target_pairs={{0,48},{16,0},{32,16},{48,32},{1,49},{17,1},{33,17},{49,33},{2,50}... | collective-permute-start | bytes 786440 | tf_op jit(solution)/shard_map/ppermute | solution.py:234
  62.8 0.0 collective-permute-done.2.refs_0_
  62.8 0.0 collective-permute-start.13
  62.8 0.0 collective-permute-done.3.refs_1_
  62.8 2.9 %collective-permute-start.14 = (bf16[128,1536]{1,0:T(8,128)(2,1)}, bf16[128,1536]{1,0:T(8,128)(2,1)S(1)}, u32[]{:S(2)}, u32[]{:S(2)}) collective-permute-start(bf16[128,1536]{1,0:T(8,128)(2,1)} %get-tuple-element.115), channel_id=1, source_target_pairs={{0,3},{1,2},{2,5},{3,4},{4,7},{5,6},{6,1},{7,0},{8,11},{9,10},{10,... | collective-permute-start | bytes 1179656 | tf_op jit(solution)/shard_map/ppermute | solution.py:243
  65.7 0.9 collective-permute-done.15.refs_1_
  66.7 4.3 %collective-permute-start.9 = (bf16[128,1536]{1,0:T(8,128)(2,1)}, bf16[128,1536]{1,0:T(8,128)(2,1)S(1)}, u32[]{:S(2)}, u32[]{:S(2)}) collective-permute-start(bf16[128,1536]{1,0:T(8,128)(2,1)} %get-tuple-element.106), channel_id=1, source_target_pairs={{0,12},{1,13},{2,14},{3,15},{4,8},{5,9},{6,10},{7,11},{8,4},{9,5},... | collective-permute-start | bytes 1179656 | tf_op jit(solution)/shard_map/ppermute | solution.py:243
  71.0 2.3 %collective-permute-done.16.refs_2_ = bf16[2,16,32,128]{3,2,1,0:T(8,128)(2,1)S(1)} collective-permute-done((bf16[2,16,32,128]{3,2,1,0:T(8,128)(2,1)S(1)}, bf16[2,16,32,128]{3,2,1,0:T(8,128)(2,1)S(1)}, u32[]{:S(2)}, u32[]{:S(2)}) %collective-permute-start.16) | collective-permute-done | bytes 262176 | tf_op jit(solution)/shard_map/ppermute | solution.py:234
  73.3 1.3 %collective-permute-start.10 = (bf16[128,1536]{1,0:T(8,128)(2,1)}, bf16[128,1536]{1,0:T(8,128)(2,1)S(1)}, u32[]{:S(2)}, u32[]{:S(2)}) collective-permute-start(bf16[128,1536]{1,0:T(8,128)(2,1)} %get-tuple-element.107), channel_id=1, source_target_pairs={{0,1},{1,0},{2,3},{3,2},{4,5},{5,4},{6,7},{7,6},{8,9},{9,8},{10,11... | collective-permute-start | bytes 1179656 | tf_op jit(solution)/shard_map/ppermute | solution.py:243
  74.5 0.0 collective-permute-done.17.refs_3_
  74.5 4.2 %collective-permute-start.4 = (bf16[128,1536]{1,0:T(8,128)(2,1)}, bf16[128,1536]{1,0:T(8,128)(2,1)S(1)}, u32[]{:S(2)}, u32[]{:S(2)}) collective-permute-start(bf16[128,1536]{1,0:T(8,128)(2,1)} %get-tuple-element.96), channel_id=1, source_target_pairs={{0,13},{1,12},{2,15},{3,14},{4,9},{5,8},{6,11},{7,10},{8,5},{9,4},... | collective-permute-start | bytes 1179656 | tf_op jit(solution)/shard_map/ppermute | solution.py:243
  78.8 1.2 %lay_router.1 = bf16[2048,128]{1,0:T(8,128)(2,1)} custom-call(bf16[2,16,32,128]{3,2,1,0:T(8,128)(2,1)S(1)} %bitcast.8, bf16[2,16,32,128]{3,2,1,0:T(8,128)(2,1)S(1)} %collective-permute-done.15.refs_1_, bf16[2,16,32,128]{3,2,1,0:T(8,128)(2,1)S(1)} %collective-permute-done.16.refs_2_, bf16[2,16,32,128]{3,2,1,0:T(8,128)(2,1)S(1)} %collective-permute-done.17.refs_3_), custom_call_target="tpu_custom_call" | custom-call | tf_op jit(solution)/shard_map/lay_router/pallas_call | solution.py:198
  80.0 3.6 %finish.4 = (bf16[2048,768]{1,0:T(8,128)(2,1)}, bf16[2048,768]{1,0:T(8,128)(2,1)}, f32[1,768]{1,0:T(1,128)}, f32[1,768]{1,0:T(1,128)}) custom-call(bf16[128,1536]{1,0:T(8,128)(2,1)} %copy-done.2, bf16[128,1536]{1,0:T(8,128)(2,1)} %copy-done.3, bf16[128,1536]{1,0:T(8,128)(2,1)} %copy-done.4, bf16[128,1536]{1,0:T(8,128)(2,1)} %copy-done.5, ...), custom_call_target="tpu_custom_call" | custom-call | tf_op jit(solution)/shard_map/finish/pallas_call | solution.py:170
  83.6 0.0 collective-permute-done.13.refs_2_
  83.6 0.0 collective-permute-done.14.refs_3_
  83.6 1.3 %finish.5 = (bf16[2048,768]{1,0:T(8,128)(2,1)}, bf16[2048,768]{1,0:T(8,128)(2,1)}) custom-call(bf16[128,1536]{1,0:T(8,128)(2,1)S(1)} %collective-permute-done.2.refs_0_, bf16[128,1536]{1,0:T(8,128)(2,1)S(1)} %collective-permute-done.3.refs_1_, bf16[128,1536]{1,0:T(8,128)(2,1)S(1)} %collective-permute-done.13.refs_2_, ...), custom_call_target="tpu_custom_call", output_to_operand_aliasing={{0}: (5, {}), {1}: (6, {})} | custom-call | tf_op jit(solution)/shard_map/finish/pallas_call | solution.py:170
  84.9 1.4 %collective-permute-done.9.refs_0_ = bf16[128,1536]{1,0:T(8,128)(2,1)S(1)} collective-permute-done((bf16[128,1536]{1,0:T(8,128)(2,1)}, bf16[128,1536]{1,0:T(8,128)(2,1)S(1)}, u32[]{:S(2)}, u32[]{:S(2)}) %collective-permute-start.9) | collective-permute-done | bytes 393248 | tf_op jit(solution)/shard_map/ppermute | solution.py:243
  86.3 0.0 collective-permute-done.10.refs_1_
  86.3 1.0 %finish.6 = (bf16[2048,768]{1,0:T(8,128)(2,1)}, bf16[2048,768]{1,0:T(8,128)(2,1)}) custom-call(bf16[128,1536]{1,0:T(8,128)(2,1)S(1)} %collective-permute-done.9.refs_0_, bf16[128,1536]{1,0:T(8,128)(2,1)S(1)} %collective-permute-done.10.refs_1_, ...), custom_call_target="tpu_custom_call", output_to_operand_aliasing={{0}: (3, {}), {1}: (4, {})} | custom-call | tf_op jit(solution)/shard_map/finish/pallas_call | solution.py:170
  87.3 8.6 %collective-permute-done.4.refs_0_ = bf16[128,1536]{1,0:T(8,128)(2,1)S(1)} collective-permute-done((bf16[128,1536]{1,0:T(8,128)(2,1)}, bf16[128,1536]{1,0:T(8,128)(2,1)S(1)}, u32[]{:S(2)}, u32[]{:S(2)}) %collective-permute-start.4) | collective-permute-done | bytes 393248 | tf_op jit(solution)/shard_map/ppermute | solution.py:243
  95.9 0.8 finish.7
  (21 shorter events, 0.0 us)
Async XLA Ops:
  3.2 18.7 %collective-permute-start.5 = (bf16[128,1536]{1,0:T(8,128)(2,1)}, bf16[128,1536]{1,0:T(8,128)(2,1)S(1)}, u32[]{:S(2)}, u32[]{:S(2)}) collective-permute-start(bf16[128,1536]{1,0:T(8,128)(2,1)} %get-tuple-element.102), channel_id=1, source_target_pairs={{0,8},{1,9},{2,10},{3,11},{4,12},{5,13},{6,14},{7,15},{8,0},{9,1},... | collective-permute-start | bytes 1179656 | tf_op jit(solution)/shard_map/ppermute | solution.py:243
  7.7 16.6 %collective-permute-start.6 = (bf16[128,1536]{1,0:T(8,128)(2,1)}, bf16[128,1536]{1,0:T(8,128)(2,1)S(1)}, u32[]{:S(2)}, u32[]{:S(2)}) collective-permute-start(bf16[128,1536]{1,0:T(8,128)(2,1)} %get-tuple-element.103), channel_id=1, source_target_pairs={{0,4},{1,5},{2,6},{3,7},{4,0},{5,1},{6,2},{7,3},{8,12},{9,13},{10,... | collective-permute-start | bytes 1179656 | tf_op jit(solution)/shard_map/ppermute | solution.py:243
  14.0 13.1 %collective-permute-start = (bf16[128,1536]{1,0:T(8,128)(2,1)}, bf16[128,1536]{1,0:T(8,128)(2,1)S(1)}, u32[]{:S(2)}, u32[]{:S(2)}) collective-permute-start(bf16[128,1536]{1,0:T(8,128)(2,1)} %get-tuple-element.92), channel_id=1, source_target_pairs={{0,9},{1,8},{2,11},{3,10},{4,13},{5,12},{6,15},{7,14},{8,1},{9,0},... | collective-permute-start | bytes 1179656 | tf_op jit(solution)/shard_map/ppermute | solution.py:243
  15.0 24.7 %collective-permute-start.1 = (bf16[128,1536]{1,0:T(8,128)(2,1)}, bf16[128,1536]{1,0:T(8,128)(2,1)S(1)}, u32[]{:S(2)}, u32[]{:S(2)}) collective-permute-start(bf16[128,1536]{1,0:T(8,128)(2,1)} %get-tuple-element.93), channel_id=1, source_target_pairs={{0,5},{1,4},{2,7},{3,6},{4,1},{5,0},{6,3},{7,2},{8,13},{9,12},{10,... | collective-permute-start | bytes 1179656 | tf_op jit(solution)/shard_map/ppermute | solution.py:243
  15.4 6.5 %copy-start.10 = (bf16[128,1536]{1,0:T(8,128)(2,1)S(1)}, bf16[128,1536]{1,0:T(8,128)(2,1)}, u32[]{:S(2)}) copy-start(bf16[128,1536]{1,0:T(8,128)(2,1)} %get-tuple-element.113) | copy-start | bytes 1179652
  15.4 13.6 %copy-start = (f32[128,16]{0,1:T(8,128)S(1)}, f32[128,16]{0,1:T(8,128)}, u32[]{:S(2)}) copy-start(f32[128,16]{0,1:T(8,128)} %param.10) | copy-start | bytes 24580
  15.4 13.6 %copy-start.1 = (f32[128]{0:T(128)S(1)}, f32[128]{0:T(128)}, u32[]{:S(2)}) copy-start(f32[128]{0:T(128)} %param.11) | copy-start | bytes 1540
  15.4 29.4 %collective-permute-start.11 = (bf16[128,1536]{1,0:T(8,128)(2,1)}, bf16[128,1536]{1,0:T(8,128)(2,1)S(1)}, u32[]{:S(2)}, u32[]{:S(2)}) collective-permute-start(bf16[128,1536]{1,0:T(8,128)(2,1)} %get-tuple-element.112), channel_id=1, source_target_pairs={{0,10},{1,11},{2,12},{3,13},{4,14},{5,15},{6,8},{7,9},{8,2},{9,3},... | collective-permute-start | bytes 1179656 | tf_op jit(solution)/shard_map/ppermute | solution.py:243
  21.9 12.5 %copy-start.2 = (bf16[128,1536]{1,0:T(8,128)(2,1)}, bf16[128,1536]{1,0:T(8,128)(2,1)S(1)}, u32[]{:S(2)}) copy-start(bf16[128,1536]{1,0:T(8,128)(2,1)S(1)} %collective-permute-done.5.refs_0_) | copy-start | bytes 1179652
  21.9 36.0 %collective-permute-start.12 = (bf16[128,1536]{1,0:T(8,128)(2,1)S(1)}, bf16[128,1536]{1,0:T(8,128)(2,1)S(1)}, u32[]{:S(2)}, u32[]{:S(2)}) collective-permute-start(bf16[128,1536]{1,0:T(8,128)(2,1)S(1)} %copy-done.10), channel_id=1, source_target_pairs={{0,6},{1,7},{2,0},{3,1},{4,2},{5,3},{6,4},{7,5},{8,14},{9,15},{10,... | collective-permute-start | bytes 1179656 | tf_op jit(solution)/shard_map/ppermute | solution.py:243
  24.2 10.2 %copy-start.3 = (bf16[128,1536]{1,0:T(8,128)(2,1)}, bf16[128,1536]{1,0:T(8,128)(2,1)S(1)}, u32[]{:S(2)}) copy-start(bf16[128,1536]{1,0:T(8,128)(2,1)S(1)} %collective-permute-done.6.refs_1_) | copy-start | bytes 1179652
  24.2 34.9 %collective-permute-start.7 = (bf16[128,1536]{1,0:T(8,128)(2,1)}, bf16[128,1536]{1,0:T(8,128)(2,1)}, u32[]{:S(2)}, u32[]{:S(2)}) collective-permute-start(bf16[128,1536]{1,0:T(8,128)(2,1)} %get-tuple-element.104), channel_id=1, source_target_pairs={{0,11},{1,10},{2,13},{3,12},{4,15},{5,14},{6,9},{7,8},{8,3},{9,2},... | collective-permute-start | bytes 1179656 | tf_op jit(solution)/shard_map/ppermute | solution.py:243
  27.1 7.3 %copy-start.4 = (bf16[128,1536]{1,0:T(8,128)(2,1)}, bf16[128,1536]{1,0:T(8,128)(2,1)S(1)}, u32[]{:S(2)}) copy-start(bf16[128,1536]{1,0:T(8,128)(2,1)S(1)} %collective-permute-done.refs_2_) | copy-start | bytes 1179652
  27.1 34.6 %collective-permute-start.8 = (bf16[128,1536]{1,0:T(8,128)(2,1)}, bf16[128,1536]{1,0:T(8,128)(2,1)}, u32[]{:S(2)}, u32[]{:S(2)}) collective-permute-start(bf16[128,1536]{1,0:T(8,128)(2,1)} %get-tuple-element.105), channel_id=1, source_target_pairs={{0,7},{1,6},{2,1},{3,0},{4,3},{5,2},{6,5},{7,4},{8,15},{9,14},{10,... | collective-permute-start | bytes 1179656 | tf_op jit(solution)/shard_map/ppermute | solution.py:243
  29.0 10.7 %copy-start.9 = (bf16[128,1536]{1,0:T(8,128)(2,1)S(1)}, bf16[128,1536]{1,0:T(8,128)(2,1)}, u32[]{:S(2)}) copy-start(bf16[128,1536]{1,0:T(8,128)(2,1)} %get-tuple-element.94) | copy-start | bytes 1179652
  29.0 15.8 %copy-start.8 = (bf16[128,1536]{1,0:T(8,128)(2,1)S(1)}, bf16[128,1536]{1,0:T(8,128)(2,1)}, u32[]{:S(2)}) copy-start(bf16[128,1536]{1,0:T(8,128)(2,1)} %get-tuple-element.95) | copy-start | bytes 1179652
  34.4 23.5 %all-to-all-start = ((bf16[32,32,128]{2,1,0:T(8,128)(2,1)}), bf16[32,32,128]{2,1,0:T(8,128)(2,1)S(1)}, u32[]{:S(2)}, u32[]{:S(2)}) async-start(bf16[32,32,128]{2,1,0:T(8,128)(2,1)} %get-tuple-element.97), calls=%async_computation | async-start | bytes 524288 | tf_op jit(solution)/shard_map/all_to_all | solution.py:208
  39.7 40.3 %copy-start.5 = (bf16[128,1536]{1,0:T(8,128)(2,1)}, bf16[128,1536]{1,0:T(8,128)(2,1)S(1)}, u32[]{:S(2)}) copy-start(bf16[128,1536]{1,0:T(8,128)(2,1)S(1)} %collective-permute-done.1.refs_3_) | copy-start | bytes 1179652
  39.7 23.1 %collective-permute-start.2 = (bf16[128,1536]{1,0:T(8,128)(2,1)S(1)}, bf16[128,1536]{1,0:T(8,128)(2,1)S(1)}, u32[]{:S(2)}, u32[]{:S(2)}) collective-permute-start(bf16[128,1536]{1,0:T(8,128)(2,1)S(1)} %copy-done.9), channel_id=1, source_target_pairs={{0,14},{1,15},{2,8},{3,9},{4,10},{5,11},{6,12},{7,13},{8,6},{9,7},... | collective-permute-start | bytes 1179656 | tf_op jit(solution)/shard_map/ppermute | solution.py:243
  44.8 35.2 %copy-start.6 = (bf16[128,1536]{1,0:T(8,128)(2,1)}, bf16[128,1536]{1,0:T(8,128)(2,1)S(1)}, u32[]{:S(2)}) copy-start(bf16[128,1536]{1,0:T(8,128)(2,1)S(1)} %collective-permute-done.11.refs_4_) | copy-start | bytes 1179652
  44.8 18.0 %collective-permute-start.3 = (bf16[128,1536]{1,0:T(8,128)(2,1)S(1)}, bf16[128,1536]{1,0:T(8,128)(2,1)S(1)}, u32[]{:S(2)}, u32[]{:S(2)}) collective-permute-start(bf16[128,1536]{1,0:T(8,128)(2,1)S(1)} %copy-done.8), channel_id=1, source_target_pairs={{0,2},{1,3},{2,4},{3,5},{4,6},{5,7},{6,0},{7,1},{8,10},{9,11},{10,... | collective-permute-start | bytes 1179656 | tf_op jit(solution)/shard_map/ppermute | solution.py:243
  58.0 22.0 %copy-start.7 = (bf16[128,1536]{1,0:T(8,128)(2,1)}, bf16[128,1536]{1,0:T(8,128)(2,1)S(1)}, u32[]{:S(2)}) copy-start(bf16[128,1536]{1,0:T(8,128)(2,1)S(1)} %collective-permute-done.12.refs_5_) | copy-start | bytes 1179652
  58.0 8.7 %collective-permute-start.15 = (bf16[2,16,32,128]{3,2,1,0:T(8,128)(2,1)S(1)}, bf16[2,16,32,128]{3,2,1,0:T(8,128)(2,1)S(1)}, u32[]{:S(2)}, u32[]{:S(2)}) collective-permute-start(bf16[2,16,32,128]{3,2,1,0:T(8,128)(2,1)S(1)} %bitcast.5), channel_id=1, source_target_pairs={{0,16},{16,32},{32,48},{48,0},{1,17},{17,33},{33,49},{49,1},{2,18}... | collective-permute-start | bytes 786440 | tf_op jit(solution)/shard_map/ppermute | solution.py:234
  59.2 14.1 %collective-permute-start.16 = (bf16[2,16,32,128]{3,2,1,0:T(8,128)(2,1)S(1)}, bf16[2,16,32,128]{3,2,1,0:T(8,128)(2,1)S(1)}, u32[]{:S(2)}, u32[]{:S(2)}) collective-permute-start(bf16[2,16,32,128]{3,2,1,0:T(8,128)(2,1)S(1)} %bitcast.6), channel_id=1, source_target_pairs={{0,32},{16,48},{32,0},{48,16},{1,33},{17,49},{33,1},{49,17},{2,34}... | collective-permute-start | bytes 786440 | tf_op jit(solution)/shard_map/ppermute | solution.py:234
  61.6 12.9 %collective-permute-start.17 = (bf16[2,16,32,128]{3,2,1,0:T(8,128)(2,1)S(1)}, bf16[2,16,32,128]{3,2,1,0:T(8,128)(2,1)S(1)}, u32[]{:S(2)}, u32[]{:S(2)}) collective-permute-start(bf16[2,16,32,128]{3,2,1,0:T(8,128)(2,1)S(1)} %bitcast.7), channel_id=1, source_target_pairs={{0,48},{16,0},{32,16},{48,32},{1,49},{17,1},{33,17},{49,33},{2,50}... | collective-permute-start | bytes 786440 | tf_op jit(solution)/shard_map/ppermute | solution.py:234
  62.8 20.8 %collective-permute-start.13 = (bf16[128,1536]{1,0:T(8,128)(2,1)}, bf16[128,1536]{1,0:T(8,128)(2,1)S(1)}, u32[]{:S(2)}, u32[]{:S(2)}) collective-permute-start(bf16[128,1536]{1,0:T(8,128)(2,1)} %get-tuple-element.114), channel_id=1, source_target_pairs={{0,15},{1,14},{2,9},{3,8},{4,11},{5,10},{6,13},{7,12},{8,7},{9,6},... | collective-permute-start | bytes 1179656 | tf_op jit(solution)/shard_map/ppermute | solution.py:243
  62.8 20.8 %collective-permute-start.14 = (bf16[128,1536]{1,0:T(8,128)(2,1)}, bf16[128,1536]{1,0:T(8,128)(2,1)S(1)}, u32[]{:S(2)}, u32[]{:S(2)}) collective-permute-start(bf16[128,1536]{1,0:T(8,128)(2,1)} %get-tuple-element.115), channel_id=1, source_target_pairs={{0,3},{1,2},{2,5},{3,4},{4,7},{5,6},{6,1},{7,0},{8,11},{9,10},{10,... | collective-permute-start | bytes 1179656 | tf_op jit(solution)/shard_map/ppermute | solution.py:243
  66.7 19.6 %collective-permute-start.9 = (bf16[128,1536]{1,0:T(8,128)(2,1)}, bf16[128,1536]{1,0:T(8,128)(2,1)S(1)}, u32[]{:S(2)}, u32[]{:S(2)}) collective-permute-start(bf16[128,1536]{1,0:T(8,128)(2,1)} %get-tuple-element.106), channel_id=1, source_target_pairs={{0,12},{1,13},{2,14},{3,15},{4,8},{5,9},{6,10},{7,11},{8,4},{9,5},... | collective-permute-start | bytes 1179656 | tf_op jit(solution)/shard_map/ppermute | solution.py:243
  73.3 13.0 %collective-permute-start.10 = (bf16[128,1536]{1,0:T(8,128)(2,1)}, bf16[128,1536]{1,0:T(8,128)(2,1)S(1)}, u32[]{:S(2)}, u32[]{:S(2)}) collective-permute-start(bf16[128,1536]{1,0:T(8,128)(2,1)} %get-tuple-element.107), channel_id=1, source_target_pairs={{0,1},{1,0},{2,3},{3,2},{4,5},{5,4},{6,7},{7,6},{8,9},{9,8},{10,11... | collective-permute-start | bytes 1179656 | tf_op jit(solution)/shard_map/ppermute | solution.py:243
  74.5 21.4 %collective-permute-start.4 = (bf16[128,1536]{1,0:T(8,128)(2,1)}, bf16[128,1536]{1,0:T(8,128)(2,1)S(1)}, u32[]{:S(2)}, u32[]{:S(2)}) collective-permute-start(bf16[128,1536]{1,0:T(8,128)(2,1)} %get-tuple-element.96), channel_id=1, source_target_pairs={{0,13},{1,12},{2,15},{3,14},{4,9},{5,8},{6,11},{7,10},{8,5},{9,4},... | collective-permute-start | bytes 1179656 | tf_op jit(solution)/shard_map/ppermute | solution.py:243

commit v2 on v1

--- a/solution.py
+++ b/solution.py
@@ -15,23 +15,23 @@
 SHARD = ("zh", "y", "c")
 GROUPS = ("zl", "zh", "y", "c")
 ROUNDS = (
+    ((1, 0, 1), (0, 2, 1)),
     ((1, 0, 0), (0, 2, 0)),
-    ((1, 0, 1), (0, 2, 1)),
+    ((1, 1, 1), (0, 3, 1)),
     ((1, 1, 0), (0, 3, 0)),
-    ((1, 1, 1), (0, 3, 1)),
+    ((1, 3, 1), (0, 1, 1)),
     ((1, 3, 0), (0, 1, 0)),
-    ((1, 3, 1), (0, 1, 1)),
     ((1, 2, 0), (0, 0, 1)),
     ((1, 2, 1), (0, 0, 0)),
 )
 BATCHES = ((0,), (1, 2), (3, 4), (5, 6, 7))
 FINALS = (
     (((0, 0), (0, 1), (1, 0), (1, 1), (2, 0), (2, 1), (3, 0), (3, 1), (7, 1)), False),
-    (((4, 0), (4, 1), (5, 0), (5, 1)), True),
-    (((6, 0), (6, 1)), True),
-    (((7, 0),), True),
+    (((4, 0), (4, 1)), True),
+    (((5, 0), (5, 1), (6, 0), (6, 1), (7, 0)), True),
 )
 DEPTH = 3
+NEAR = (0, 1, 2)
 ANY = pl.BlockSpec(memory_space=pltpu.HBM)
 VMEM = pl.BlockSpec(memory_space=pltpu.VMEM)
 
@@ -55,7 +55,7 @@
     return pltpu.CompilerParams(vmem_limit_bytes=mib << 20)
 
 
-def merge_chunks(steps, arrays, earlier=None, router=None):
+def merge_chunks(steps, arrays, earlier=None, router=None, near=False):
     _, rows, cols = arrays[0].shape
     n = len(steps)
     last = earlier is not None
@@ -87,7 +87,8 @@
                 for c in copies[k][2 * h : 2 * h + 2]:
                     c.wait()
                 m = bufs[2 * h][k] + bufs[2 * h + 1][k].astype(jnp.float32)
-                obuf[k, :, h * cols : (h + 1) * cols] = m.astype(jnp.bfloat16)
+                to = o if near else obuf.at[k]
+                to[:, h * cols : (h + 1) * cols] = m.astype(jnp.bfloat16)
                 t = jnp.abs(m).reshape(rows // 8, 8, cols).sum(0).sum(0, keepdims=True)
                 for j in range(cols // LANES):
                     at = h * (cols // LANES) + j
@@ -95,8 +96,9 @@
                         pay[place(steps[k], 1), at : at + 1, :] = t[:, j * LANES : (j + 1) * LANES]
                     else:
                         sums[k, at : at + 1, :] = t[:, j * LANES : (j + 1) * LANES]
-            sent.append(pltpu.make_async_copy(obuf.at[k], o, osem.at[k]))
-            sent[-1].start()
+            if not near:
+                sent.append(pltpu.make_async_copy(obuf.at[k], o, osem.at[k]))
+                sent[-1].start()
         if last:
             r = part.shape[0]
             tail = pay[...].astype(jnp.bfloat16)
@@ -116,10 +118,10 @@
     return pl.pallas_call(
         body,
         in_specs=[ANY] * 4 + [VMEM] * len(old),
-        out_specs=[ANY] * n + [VMEM],
-        out_shape=[pltpu.HBM((rows, 2 * cols), jnp.bfloat16)] * n + [extra],
+        out_specs=[VMEM if near else ANY] * n + [VMEM],
+        out_shape=[(pltpu.VMEM if near else pltpu.HBM)((rows, 2 * cols), jnp.bfloat16)] * n + [extra],
         scratch_shapes=[pltpu.VMEM((n, rows, cols), a.dtype) for a in arrays]
-        + [pltpu.VMEM((n, rows, 2 * cols), jnp.bfloat16), pltpu.SemaphoreType.DMA((n, 4)), pltpu.SemaphoreType.DMA((n,)), pay],
+        + [pltpu.VMEM((1 if near else n, rows, 2 * cols), jnp.bfloat16), pltpu.SemaphoreType.DMA((n, 4)), pltpu.SemaphoreType.DMA((n,)), pay],
         compiler_params=params((size >> 20) + 3),
         name="merge",
     )(*[in_hbm(a) for a in arrays], *old)
@@ -182,7 +184,6 @@
 
 def lay_router(groups):
     _, s, e, rows = groups[0].shape
-    e //= 2
     m = len(groups)
 
     def body(*refs):
@@ -192,7 +193,7 @@
             for d in range(m):
                 for w in range(2):
                     at = (w * m + lax.rem(x + m - d, m)) * e
-                    buf[k, pl.ds(pl.multiple_of(at, e), e), :] = refs[d][w, k, :e, :].astype(jnp.float32)
+                    buf[k, pl.ds(pl.multiple_of(at, e), e), :] = refs[d][w, k].astype(jnp.float32)
             o_ref[k * rows : (k + 1) * rows, :] = buf[k].T.astype(jnp.bfloat16)
 
     return pl.pallas_call(
@@ -219,7 +220,7 @@
     for b, batch in enumerate(BATCHES):
         steps = [s for r in batch for s in ROUNDS[r]]
         last = b == len(BATCHES) - 1
-        *made, part_sums = merge_chunks(steps, arrays, *((sums, (router_weight.T, router_gain[None])) if last else ()))
+        *made, part_sums = merge_chunks(steps, arrays, *((sums, (router_weight.T, router_gain[None])) if last else (None, None)), near=b in NEAR)
         sums.append((steps, part_sums))
         if not last:
             arrays, (made[0],) = tied(arrays, [made[0]])
@@ -227,7 +228,7 @@
             chunks.append(made[: len(ROUNDS[r])])
             made = made[len(ROUNDS[r]) :]
     small = exchange(sums[-1][1], GROUPS)
-    cols = small.reshape(2, 16, *small.shape[1:])
+    cols = small[:, : small.shape[1] // 2].reshape(2, 16, -1, small.shape[2])
     m = lax.axis_size("x")
     groups = [cols]
     for d in range(1, m):

time: 97 us -> 96.6 us (level)
  blocking collectives: 0 us -> 14.8 us
  starting transfers between devices: 44.4 us -> 38 us
  waiting for transfers between devices: 28.7 us -> 24 us
  Pallas kernels: 22.8 us -> 18.7 us
    all_to_all x0 -> x1, blocking collectives: none -> 14.8 us  [exchange(): return lax.all_to_all(x, axes, 0, 0, tiled=True)]
    all_to_all x1 -> x0, waiting for transfers between devices: 13.1 us -> none  [exchange(): return lax.all_to_all(x, axes, 0, 0, tiled=True)]
    ppermute x15, waiting for transfers between devices: 12.4 us -> 24 us  [shards(): moved.append(lax.ppermute(v, SHARD, ring(s)) if any(s) else v)]
    all_to_all x1 -> x0, starting transfers between devices: 5.28 us -> none  [exchange(): return lax.all_to_all(x, axes, 0, 0, tiled=True)]
    pallas_call x4, Pallas kernels: 14.8 us -> 11.5 us  [merge_chunks(): pl.pallas_call(body, in_specs=[ANY] * 4 + [VMEM] * len(old), out_specs=[V...]
    ppermute x3, waiting for transfers between devices: 3.18 us -> 0.01 us  [shards(): groups.append(lax.ppermute(cols, 'x', [(i, (i + d) % m) for i in range(m)]))]
    ppermute x15, starting transfers between devices: 34.3 us -> 33.1 us  [shards(): moved.append(lax.ppermute(v, SHARD, ring(s)) if any(s) else v)]
    pallas_call x4 -> x3, Pallas kernels: 6.71 us -> 6.03 us  [finish(): pl.pallas_call(body, in_specs=[pl.BlockSpec(memory_space=space)] * n + [V...]
  transfers between devices with their start and end apart: 19 -> 18, of which waited for: 6 -> 5; matrix products, arithmetic and copies ran while one was open for 0% -> 0% of each run, Pallas kernels for 20% -> 16%
where the time goes in v2:
time: 96.6 us; the launch traced here: 96.4 us
  starting transfers between devices  38 us (39%)
  waiting for transfers between devices  24 us (25%)
  Pallas kernels  18.7 us (19%)
  blocking collectives  14.8 us (15%)
    ppermute x15, starting transfers between devices, shards(): moved.append(lax.ppermute(v, SHARD, ring(s)) if any(s) else v)  33.1 us
    ppermute x15, waiting for transfers between devices, shards(): moved.append(lax.ppermute(v, SHARD, ring(s)) if any(s) else v)  24 us
    all_to_all x1, blocking collectives, exchange(): return lax.all_to_all(x, axes, 0, 0, tiled=True)  14.8 us
    pallas_call x4, Pallas kernels, merge_chunks(): pl.pallas_call(body, in_specs=[ANY] * 4 + [VMEM] * len(old), out_specs=[V...  11.5 us
    pallas_call x3, Pallas kernels, finish(): pl.pallas_call(body, in_specs=[pl.BlockSpec(memory_space=space)] * n + [V...  6.03 us
    ppermute x3, starting transfers between devices, shards(): groups.append(lax.ppermute(cols, 'x', [(i, (i + d) % m) for i in range(m)]))  4.88 us
  transfers between devices with their start and end apart: 18, of which 5 were waited for; matrix products, arithmetic and copies ran while one was open for 0% of the time, Pallas kernels for 16%

profile of v2, /device:TPU:1, one launch (start us, length us, event | category | flops | bytes accessed | tf_op | source)
XLA Modules:
  0.0 96.4 jit_solution(7276638773473171108)
XLA Ops:
  0.6 1.8 %merge.4 = (bf16[128,1536]{1,0:T(8,128)(2,1)S(1)}, bf16[128,1536]{1,0:T(8,128)(2,1)S(1)}, f32[2,12,128]{2,1,0:T(8,128)S(1)}) custom-call(f32[16,128,768]{2,1,0:T(8,128)} %refs_0_.4, bf16[16,128,768]{2,1,0:T(8,128)(2,1)} %refs_1_.4, f32[16,128,768]{2,1,0:T(8,128)} %refs_2_.4, bf16[16,128,768]{2,1,0:T(8,128)(2,1)} %refs_3_.4), custom_call_target="tpu_custom_call" | custom-call | tf_op jit(solution)/shard_map/merge/pallas_call | solution.py:118
  2.4 5.1 %collective-permute-start.4 = (bf16[128,1536]{1,0:T(8,128)(2,1)S(1)}, bf16[128,1536]{1,0:T(8,128)(2,1)S(1)}, u32[]{:S(2)}, u32[]{:S(2)}) collective-permute-start(bf16[128,1536]{1,0:T(8,128)(2,1)S(1)} %get-tuple-element.96), channel_id=1, source_target_pairs={{0,9},{1,8},{2,11},{3,10},{4,13},{5,12},{6,15},{7,14},{8,1},{9,0},... | collective-permute-start | bytes 1179656 | tf_op jit(solution)/shard_map/ppermute | solution.py:244
  7.5 2.6 %collective-permute-start.5 = (bf16[128,1536]{1,0:T(8,128)(2,1)S(1)}, bf16[128,1536]{1,0:T(8,128)(2,1)S(1)}, u32[]{:S(2)}, u32[]{:S(2)}) collective-permute-start(bf16[128,1536]{1,0:T(8,128)(2,1)S(1)} %get-tuple-element.97), channel_id=1, source_target_pairs={{0,5},{1,4},{2,7},{3,6},{4,1},{5,0},{6,3},{7,2},{8,13},{9,12},{10,... | collective-permute-start | bytes 1179656 | tf_op jit(solution)/shard_map/ppermute | solution.py:244
  10.1 2.6 %merge.5 = (bf16[128,1536]{1,0:T(8,128)(2,1)S(1)}, bf16[128,1536]{1,0:T(8,128)(2,1)S(1)}, bf16[128,1536]{1,0:T(8,128)(2,1)S(1)}, bf16[128,1536]{1,0:T(8,128)(2,1)S(1)}, f32[4,12,128]{2,1,0:T(8,128)S(1)}) custom-call(f32[16,128,768]{2,1,0:T(8,128)} %refs_0_.4, bf16[16,128,768]{2,1,0:T(8,128)(2,1)} %refs_1_.4, f32[16,128,768]{2,1,0:T(8,128)} %refs_2_.4, ...), custom_call_target="tpu_custom_call" | custom-call | tf_op jit(solution)/shard_map/merge/pallas_call | solution.py:118
  12.7 0.5 collective-permute-start.10
  13.1 0.1 collective-permute-start.11
  13.2 4.7 %collective-permute-start = (bf16[128,1536]{1,0:T(8,128)(2,1)S(1)}, bf16[128,1536]{1,0:T(8,128)(2,1)S(1)}, u32[]{:S(2)}, u32[]{:S(2)}) collective-permute-start(bf16[128,1536]{1,0:T(8,128)(2,1)S(1)} %get-tuple-element.88), channel_id=1, source_target_pairs={{0,11},{1,10},{2,13},{3,12},{4,15},{5,14},{6,9},{7,8},{8,3},{9,2},... | collective-permute-start | bytes 1179656 | tf_op jit(solution)/shard_map/ppermute | solution.py:244
  17.9 2.6 %merge.6 = (bf16[128,1536]{1,0:T(8,128)(2,1)S(1)}, bf16[128,1536]{1,0:T(8,128)(2,1)S(1)}, bf16[128,1536]{1,0:T(8,128)(2,1)S(1)}, bf16[128,1536]{1,0:T(8,128)(2,1)S(1)}, f32[4,12,128]{2,1,0:T(8,128)S(1)}) custom-call(f32[16,128,768]{2,1,0:T(8,128)} %refs_0_.4, bf16[16,128,768]{2,1,0:T(8,128)(2,1)} %refs_1_.4, f32[16,128,768]{2,1,0:T(8,128)} %refs_2_.4, ...), custom_call_target="tpu_custom_call" | custom-call | tf_op jit(solution)/shard_map/merge/pallas_call | solution.py:118
  20.5 0.0 collective-permute-done.4.refs_0_
  20.5 0.0 copy-start.2
  20.5 0.8 collective-permute-start.1
  21.4 0.0 collective-permute-done.5.refs_1_
  21.4 0.2 collective-permute-start.6
  21.6 3.3 %collective-permute-done.10.refs_2_ = bf16[128,1536]{1,0:T(8,128)(2,1)S(1)} collective-permute-done((bf16[128,1536]{1,0:T(8,128)(2,1)S(1)}, bf16[128,1536]{1,0:T(8,128)(2,1)S(1)}, u32[]{:S(2)}, u32[]{:S(2)}) %collective-permute-start.10) | collective-permute-done | bytes 393248 | tf_op jit(solution)/shard_map/ppermute | solution.py:244
  24.9 2.5 %collective-permute-start.7 = (bf16[128,1536]{1,0:T(8,128)(2,1)S(1)}, bf16[128,1536]{1,0:T(8,128)(2,1)S(1)}, u32[]{:S(2)}, u32[]{:S(2)}) collective-permute-start(bf16[128,1536]{1,0:T(8,128)(2,1)S(1)} %get-tuple-element.99), channel_id=1, source_target_pairs={{0,6},{1,7},{2,0},{3,1},{4,2},{5,3},{6,4},{7,5},{8,14},{9,15},{10,... | collective-permute-start | bytes 1179656 | tf_op jit(solution)/shard_map/ppermute | solution.py:244
  27.4 0.5 collective-permute-done.11.refs_3_
  27.9 4.2 %collective-permute-start.12 = (bf16[128,1536]{1,0:T(8,128)(2,1)S(1)}, bf16[128,1536]{1,0:T(8,128)(2,1)S(1)}, u32[]{:S(2)}, u32[]{:S(2)}) collective-permute-start(bf16[128,1536]{1,0:T(8,128)(2,1)S(1)} %get-tuple-element.108), channel_id=1, source_target_pairs={{0,15},{1,14},{2,9},{3,8},{4,11},{5,10},{6,13},{7,12},{8,7},{9,6},... | collective-permute-start | bytes 1179656 | tf_op jit(solution)/shard_map/ppermute | solution.py:244
  32.1 4.6 %collective-permute-done.refs_4_ = bf16[128,1536]{1,0:T(8,128)(2,1)S(1)} collective-permute-done((bf16[128,1536]{1,0:T(8,128)(2,1)S(1)}, bf16[128,1536]{1,0:T(8,128)(2,1)S(1)}, u32[]{:S(2)}, u32[]{:S(2)}) %collective-permute-start) | collective-permute-done | bytes 393248 | tf_op jit(solution)/shard_map/ppermute | solution.py:244
  36.7 1.8 %collective-permute-start.13 = (bf16[128,1536]{1,0:T(8,128)(2,1)S(1)}, bf16[128,1536]{1,0:T(8,128)(2,1)S(1)}, u32[]{:S(2)}, u32[]{:S(2)}) collective-permute-start(bf16[128,1536]{1,0:T(8,128)(2,1)S(1)} %get-tuple-element.109), channel_id=1, source_target_pairs={{0,3},{1,2},{2,5},{3,4},{4,7},{5,6},{6,1},{7,0},{8,11},{9,10},{10,... | collective-permute-start | bytes 1179656 | tf_op jit(solution)/shard_map/ppermute | solution.py:244
  38.5 0.0 copy-done.1
  38.5 4.6 %merge.7 = (bf16[128,1536]{1,0:T(8,128)(2,1)}, bf16[128,1536]{1,0:T(8,128)(2,1)}, bf16[128,1536]{1,0:T(8,128)(2,1)}, bf16[128,1536]{1,0:T(8,128)(2,1)}, bf16[128...) custom-call(f32[16,128,768]{2,1,0:T(8,128)} %refs_0_.4, ...), custom_call_target="tpu_custom_call" | custom-call | tf_op jit(solution)/shard_map/merge/pallas_call | solution.py:118
  43.2 14.8 %all_to_all.5.refs_9_.refs_2_.refs_5_ = bf16[32,32,128]{2,1,0:T(8,128)(2,1)S(1)} all-to-all(bf16[32,32,128]{2,1,0:T(8,128)(2,1)S(1)} %get-tuple-element.111), channel_id=1, replica_groups=mesh['zl'=2,'x'=4,'zh'=2,'y'=4,'c'=2] {'zl','zh','y','c'}, dimensions={0} | all-to-all | bytes 524288 | tf_op jit(solution)/shard_map/all_to_all | solution.py:209
  58.0 0.0 collective-permute-done.1.refs_5_
  58.0 0.0 copy-start.7
  58.0 1.3 %collective-permute-start.15 = (bf16[2,16,16,128]{3,2,1,0:T(8,128)(2,1)S(1)}, bf16[2,16,16,128]{3,2,1,0:T(8,128)(2,1)S(1)}, u32[]{:S(2)}, u32[]{:S(2)}) collective-permute-start(bf16[2,16,16,128]{3,2,1,0:T(8,128)(2,1)S(1)} %bitcast.5), channel_id=1, source_target_pairs={{0,16},{16,32},{32,48},{48,0},{1,17},{17,33},{33,49},{49,1},{2,18}... | collective-permute-start | bytes 393224 | tf_op jit(solution)/shard_map/ppermute | solution.py:235
  59.3 0.0 collective-permute-done.6.refs_6_
  59.3 2.5 %collective-permute-start.16 = (bf16[2,16,16,128]{3,2,1,0:T(8,128)(2,1)S(1)}, bf16[2,16,16,128]{3,2,1,0:T(8,128)(2,1)S(1)}, u32[]{:S(2)}, u32[]{:S(2)}) collective-permute-start(bf16[2,16,16,128]{3,2,1,0:T(8,128)(2,1)S(1)} %bitcast.6), channel_id=1, source_target_pairs={{0,32},{16,48},{32,0},{48,16},{1,33},{17,49},{33,1},{49,17},{2,34}... | collective-permute-start | bytes 393224 | tf_op jit(solution)/shard_map/ppermute | solution.py:235
  61.7 0.0 collective-permute-done.7.refs_7_
  61.7 1.2 %collective-permute-start.17 = (bf16[2,16,16,128]{3,2,1,0:T(8,128)(2,1)S(1)}, bf16[2,16,16,128]{3,2,1,0:T(8,128)(2,1)S(1)}, u32[]{:S(2)}, u32[]{:S(2)}) collective-permute-start(bf16[2,16,16,128]{3,2,1,0:T(8,128)(2,1)S(1)} %bitcast.7), channel_id=1, source_target_pairs={{0,48},{16,0},{32,16},{48,32},{1,49},{17,1},{33,17},{49,33},{2,50}... | collective-permute-start | bytes 393224 | tf_op jit(solution)/shard_map/ppermute | solution.py:235
  62.9 0.0 collective-permute-done.12.refs_0_
  62.9 3.4 %collective-permute-start.2 = (bf16[128,1536]{1,0:T(8,128)(2,1)}, bf16[128,1536]{1,0:T(8,128)(2,1)S(1)}, u32[]{:S(2)}, u32[]{:S(2)}) collective-permute-start(bf16[128,1536]{1,0:T(8,128)(2,1)} %get-tuple-element.90), channel_id=1, source_target_pairs={{0,14},{1,15},{2,8},{3,9},{4,10},{5,11},{6,12},{7,13},{8,6},{9,7},... | collective-permute-start | bytes 1179656 | tf_op jit(solution)/shard_map/ppermute | solution.py:244
  66.3 0.0 collective-permute-done.13.refs_1_
  66.3 0.0 collective-permute-start.3
  66.3 0.0 collective-permute-done.15.refs_1_
  66.3 2.2 %collective-permute-start.8 = (bf16[128,1536]{1,0:T(8,128)(2,1)}, bf16[128,1536]{1,0:T(8,128)(2,1)S(1)}, u32[]{:S(2)}, u32[]{:S(2)}) collective-permute-start(bf16[128,1536]{1,0:T(8,128)(2,1)} %get-tuple-element.100), channel_id=1, source_target_pairs={{0,12},{1,13},{2,14},{3,15},{4,8},{5,9},{6,10},{7,11},{8,4},{9,5},... | collective-permute-start | bytes 1179656 | tf_op jit(solution)/shard_map/ppermute | solution.py:244
  68.5 0.0 collective-permute-done.16.refs_2_
  68.5 2.0 %collective-permute-start.9 = (bf16[128,1536]{1,0:T(8,128)(2,1)}, bf16[128,1536]{1,0:T(8,128)(2,1)S(1)}, u32[]{:S(2)}, u32[]{:S(2)}) collective-permute-start(bf16[128,1536]{1,0:T(8,128)(2,1)} %get-tuple-element.101), channel_id=1, source_target_pairs={{0,1},{1,0},{2,3},{3,2},{4,5},{5,4},{6,7},{7,6},{8,9},{9,8},{10,11... | collective-permute-start | bytes 1179656 | tf_op jit(solution)/shard_map/ppermute | solution.py:244
  70.5 0.0 collective-permute-done.17.refs_3_
  70.5 3.0 %collective-permute-start.14 = (bf16[128,1536]{1,0:T(8,128)(2,1)}, bf16[128,1536]{1,0:T(8,128)(2,1)S(1)}, u32[]{:S(2)}, u32[]{:S(2)}) collective-permute-start(bf16[128,1536]{1,0:T(8,128)(2,1)} %get-tuple-element.110), channel_id=1, source_target_pairs={{0,13},{1,12},{2,15},{3,14},{4,9},{5,8},{6,11},{7,10},{8,5},{9,4},... | collective-permute-start | bytes 1179656 | tf_op jit(solution)/shard_map/ppermute | solution.py:244
  73.5 1.2 %lay_router.1 = bf16[2048,128]{1,0:T(8,128)(2,1)} custom-call(bf16[2,16,16,128]{3,2,1,0:T(8,128)(2,1)S(1)} %bitcast.8, bf16[2,16,16,128]{3,2,1,0:T(8,128)(2,1)S(1)} %collective-permute-done.15.refs_1_, bf16[2,16,16,128]{3,2,1,0:T(8,128)(2,1)S(1)} %collective-permute-done.16.refs_2_, bf16[2,16,16,128]{3,2,1,0:T(8,128)(2,1)S(1)} %collective-permute-done.17.refs_3_), custom_call_target="tpu_custom_call" | custom-call | tf_op jit(solution)/shard_map/lay_router/pallas_call | solution.py:199
  74.7 3.6 %finish.3 = (bf16[2048,768]{1,0:T(8,128)(2,1)}, bf16[2048,768]{1,0:T(8,128)(2,1)}, f32[1,768]{1,0:T(1,128)}, f32[1,768]{1,0:T(1,128)}) custom-call(bf16[128,1536]{1,0:T(8,128)(2,1)} %copy-done.2, bf16[128,1536]{1,0:T(8,128)(2,1)} %copy-done.3, bf16[128,1536]{1,0:T(8,128)(2,1)} %copy-done.4, bf16[128,1536]{1,0:T(8,128)(2,1)} %copy-done.5, ...), custom_call_target="tpu_custom_call" | custom-call | tf_op jit(solution)/shard_map/finish/pallas_call | solution.py:172
  78.4 1.0 %finish.4 = (bf16[2048,768]{1,0:T(8,128)(2,1)}, bf16[2048,768]{1,0:T(8,128)(2,1)}) custom-call(bf16[128,1536]{1,0:T(8,128)(2,1)S(1)} %collective-permute-done.12.refs_0_, bf16[128,1536]{1,0:T(8,128)(2,1)S(1)} %collective-permute-done.13.refs_1_, ...), custom_call_target="tpu_custom_call", output_to_operand_aliasing={{0}: (3, {}), {1}: (4, {})} | custom-call | tf_op jit(solution)/shard_map/finish/pallas_call | solution.py:172
  79.4 0.0 collective-permute-done.2.refs_0_
  79.4 0.0 collective-permute-done.3.refs_1_
  79.4 5.5 %collective-permute-done.8.refs_2_ = bf16[128,1536]{1,0:T(8,128)(2,1)S(1)} collective-permute-done((bf16[128,1536]{1,0:T(8,128)(2,1)}, bf16[128,1536]{1,0:T(8,128)(2,1)S(1)}, u32[]{:S(2)}, u32[]{:S(2)}) %collective-permute-start.8) | collective-permute-done | bytes 393248 | tf_op jit(solution)/shard_map/ppermute | solution.py:244
  84.9 0.0 collective-permute-done.9.refs_3_
  84.9 10.1 %collective-permute-done.14.refs_4_ = bf16[128,1536]{1,0:T(8,128)(2,1)S(1)} collective-permute-done((bf16[128,1536]{1,0:T(8,128)(2,1)}, bf16[128,1536]{1,0:T(8,128)(2,1)S(1)}, u32[]{:S(2)}, u32[]{:S(2)}) %collective-permute-start.14) | collective-permute-done | bytes 393248 | tf_op jit(solution)/shard_map/ppermute | solution.py:244
  95.0 1.4 %finish.5 = (bf16[2048,768]{1,0:T(8,128)(2,1)}, bf16[2048,768]{1,0:T(8,128)(2,1)}) custom-call(bf16[128,1536]{1,0:T(8,128)(2,1)S(1)} %collective-permute-done.2.refs_0_, bf16[128,1536]{1,0:T(8,128)(2,1)S(1)} %collective-permute-done.3.refs_1_, bf16[128,1536]{1,0:T(8,128)(2,1)S(1)} %collective-permute-done.8.refs_2_, ...), custom_call_target="tpu_custom_call", output_to_operand_aliasing={{0}: (6, {}), {1}: (7, {})} | custom-call | tf_op jit(solution)/shard_map/finish/pallas_call | solution.py:172
  (18 shorter events, 0.0 us)
Async XLA Ops:
  2.4 18.1 %collective-permute-start.4 = (bf16[128,1536]{1,0:T(8,128)(2,1)S(1)}, bf16[128,1536]{1,0:T(8,128)(2,1)S(1)}, u32[]{:S(2)}, u32[]{:S(2)}) collective-permute-start(bf16[128,1536]{1,0:T(8,128)(2,1)S(1)} %get-tuple-element.96), channel_id=1, source_target_pairs={{0,9},{1,8},{2,11},{3,10},{4,13},{5,12},{6,15},{7,14},{8,1},{9,0},... | collective-permute-start | bytes 1179656 | tf_op jit(solution)/shard_map/ppermute | solution.py:244
  7.5 13.9 %collective-permute-start.5 = (bf16[128,1536]{1,0:T(8,128)(2,1)S(1)}, bf16[128,1536]{1,0:T(8,128)(2,1)S(1)}, u32[]{:S(2)}, u32[]{:S(2)}) collective-permute-start(bf16[128,1536]{1,0:T(8,128)(2,1)S(1)} %get-tuple-element.97), channel_id=1, source_target_pairs={{0,5},{1,4},{2,7},{3,6},{4,1},{5,0},{6,3},{7,2},{8,13},{9,12},{10,... | collective-permute-start | bytes 1179656 | tf_op jit(solution)/shard_map/ppermute | solution.py:244
  12.7 12.2 %collective-permute-start.10 = (bf16[128,1536]{1,0:T(8,128)(2,1)S(1)}, bf16[128,1536]{1,0:T(8,128)(2,1)S(1)}, u32[]{:S(2)}, u32[]{:S(2)}) collective-permute-start(bf16[128,1536]{1,0:T(8,128)(2,1)S(1)} %get-tuple-element.106), channel_id=1, source_target_pairs={{0,8},{1,9},{2,10},{3,11},{4,12},{5,13},{6,14},{7,15},{8,0},{9,1},... | collective-permute-start | bytes 1179656 | tf_op jit(solution)/shard_map/ppermute | solution.py:244
  13.1 14.8 %collective-permute-start.11 = (bf16[128,1536]{1,0:T(8,128)(2,1)S(1)}, bf16[128,1536]{1,0:T(8,128)(2,1)S(1)}, u32[]{:S(2)}, u32[]{:S(2)}) collective-permute-start(bf16[128,1536]{1,0:T(8,128)(2,1)S(1)} %get-tuple-element.107), channel_id=1, source_target_pairs={{0,4},{1,5},{2,6},{3,7},{4,0},{5,1},{6,2},{7,3},{8,12},{9,13},{10,... | collective-permute-start | bytes 1179656 | tf_op jit(solution)/shard_map/ppermute | solution.py:244
  13.2 25.3 %copy-start = (f32[128,16]{0,1:T(8,128)S(1)}, f32[128,16]{0,1:T(8,128)}, u32[]{:S(2)}) copy-start(f32[128,16]{0,1:T(8,128)} %param.10) | copy-start | bytes 24580
  13.2 25.3 %copy-start.1 = (f32[128]{0:T(128)S(1)}, f32[128]{0:T(128)}, u32[]{:S(2)}) copy-start(f32[128]{0:T(128)} %param.11) | copy-start | bytes 1540
  13.2 23.5 %collective-permute-start = (bf16[128,1536]{1,0:T(8,128)(2,1)S(1)}, bf16[128,1536]{1,0:T(8,128)(2,1)S(1)}, u32[]{:S(2)}, u32[]{:S(2)}) collective-permute-start(bf16[128,1536]{1,0:T(8,128)(2,1)S(1)} %get-tuple-element.88), channel_id=1, source_target_pairs={{0,11},{1,10},{2,13},{3,12},{4,15},{5,14},{6,9},{7,8},{8,3},{9,2},... | collective-permute-start | bytes 1179656 | tf_op jit(solution)/shard_map/ppermute | solution.py:244
  20.5 22.6 %copy-start.2 = (bf16[128,1536]{1,0:T(8,128)(2,1)}, bf16[128,1536]{1,0:T(8,128)(2,1)S(1)}, u32[]{:S(2)}) copy-start(bf16[128,1536]{1,0:T(8,128)(2,1)S(1)} %collective-permute-done.4.refs_0_) | copy-start | bytes 1179652
  20.5 37.5 %collective-permute-start.1 = (bf16[128,1536]{1,0:T(8,128)(2,1)S(1)}, bf16[128,1536]{1,0:T(8,128)(2,1)S(1)}, u32[]{:S(2)}, u32[]{:S(2)}) collective-permute-start(bf16[128,1536]{1,0:T(8,128)(2,1)S(1)} %get-tuple-element.89), channel_id=1, source_target_pairs={{0,7},{1,6},{2,1},{3,0},{4,3},{5,2},{6,5},{7,4},{8,15},{9,14},{10,... | collective-permute-start | bytes 1179656 | tf_op jit(solution)/shard_map/ppermute | solution.py:244
  21.4 21.8 %copy-start.3 = (bf16[128,1536]{1,0:T(8,128)(2,1)}, bf16[128,1536]{1,0:T(8,128)(2,1)S(1)}, u32[]{:S(2)}) copy-start(bf16[128,1536]{1,0:T(8,128)(2,1)S(1)} %collective-permute-done.5.refs_1_) | copy-start | bytes 1179652
  21.4 37.9 %collective-permute-start.6 = (bf16[128,1536]{1,0:T(8,128)(2,1)S(1)}, bf16[128,1536]{1,0:T(8,128)(2,1)S(1)}, u32[]{:S(2)}, u32[]{:S(2)}) collective-permute-start(bf16[128,1536]{1,0:T(8,128)(2,1)S(1)} %get-tuple-element.98), channel_id=1, source_target_pairs={{0,10},{1,11},{2,12},{3,13},{4,14},{5,15},{6,8},{7,9},{8,2},{9,3},... | collective-permute-start | bytes 1179656 | tf_op jit(solution)/shard_map/ppermute | solution.py:244
  24.9 18.2 %copy-start.4 = (bf16[128,1536]{1,0:T(8,128)(2,1)}, bf16[128,1536]{1,0:T(8,128)(2,1)S(1)}, u32[]{:S(2)}) copy-start(bf16[128,1536]{1,0:T(8,128)(2,1)S(1)} %collective-permute-done.10.refs_2_) | copy-start | bytes 1179652
  24.9 36.8 %collective-permute-start.7 = (bf16[128,1536]{1,0:T(8,128)(2,1)S(1)}, bf16[128,1536]{1,0:T(8,128)(2,1)S(1)}, u32[]{:S(2)}, u32[]{:S(2)}) collective-permute-start(bf16[128,1536]{1,0:T(8,128)(2,1)S(1)} %get-tuple-element.99), channel_id=1, source_target_pairs={{0,6},{1,7},{2,0},{3,1},{4,2},{5,3},{6,4},{7,5},{8,14},{9,15},{10,... | collective-permute-start | bytes 1179656 | tf_op jit(solution)/shard_map/ppermute | solution.py:244
  27.9 15.2 %copy-start.5 = (bf16[128,1536]{1,0:T(8,128)(2,1)}, bf16[128,1536]{1,0:T(8,128)(2,1)S(1)}, u32[]{:S(2)}) copy-start(bf16[128,1536]{1,0:T(8,128)(2,1)S(1)} %collective-permute-done.11.refs_3_) | copy-start | bytes 1179652
  27.9 35.0 %collective-permute-start.12 = (bf16[128,1536]{1,0:T(8,128)(2,1)S(1)}, bf16[128,1536]{1,0:T(8,128)(2,1)S(1)}, u32[]{:S(2)}, u32[]{:S(2)}) collective-permute-start(bf16[128,1536]{1,0:T(8,128)(2,1)S(1)} %get-tuple-element.108), channel_id=1, source_target_pairs={{0,15},{1,14},{2,9},{3,8},{4,11},{5,10},{6,13},{7,12},{8,7},{9,6},... | collective-permute-start | bytes 1179656 | tf_op jit(solution)/shard_map/ppermute | solution.py:244
  36.7 6.4 %copy-start.6 = (bf16[128,1536]{1,0:T(8,128)(2,1)}, bf16[128,1536]{1,0:T(8,128)(2,1)S(1)}, u32[]{:S(2)}) copy-start(bf16[128,1536]{1,0:T(8,128)(2,1)S(1)} %collective-permute-done.refs_4_) | copy-start | bytes 1179652
  36.7 29.6 %collective-permute-start.13 = (bf16[128,1536]{1,0:T(8,128)(2,1)S(1)}, bf16[128,1536]{1,0:T(8,128)(2,1)S(1)}, u32[]{:S(2)}, u32[]{:S(2)}) collective-permute-start(bf16[128,1536]{1,0:T(8,128)(2,1)S(1)} %get-tuple-element.109), channel_id=1, source_target_pairs={{0,3},{1,2},{2,5},{3,4},{4,7},{5,6},{6,1},{7,0},{8,11},{9,10},{10,... | collective-permute-start | bytes 1179656 | tf_op jit(solution)/shard_map/ppermute | solution.py:244
  58.0 16.8 %copy-start.7 = (bf16[128,1536]{1,0:T(8,128)(2,1)}, bf16[128,1536]{1,0:T(8,128)(2,1)S(1)}, u32[]{:S(2)}) copy-start(bf16[128,1536]{1,0:T(8,128)(2,1)S(1)} %collective-permute-done.1.refs_5_) | copy-start | bytes 1179652
  58.0 8.3 %collective-permute-start.15 = (bf16[2,16,16,128]{3,2,1,0:T(8,128)(2,1)S(1)}, bf16[2,16,16,128]{3,2,1,0:T(8,128)(2,1)S(1)}, u32[]{:S(2)}, u32[]{:S(2)}) collective-permute-start(bf16[2,16,16,128]{3,2,1,0:T(8,128)(2,1)S(1)} %bitcast.5), channel_id=1, source_target_pairs={{0,16},{16,32},{32,48},{48,0},{1,17},{17,33},{33,49},{49,1},{2,18}... | collective-permute-start | bytes 393224 | tf_op jit(solution)/shard_map/ppermute | solution.py:235
  59.3 15.5 %copy-start.8 = (bf16[128,1536]{1,0:T(8,128)(2,1)}, bf16[128,1536]{1,0:T(8,128)(2,1)S(1)}, u32[]{:S(2)}) copy-start(bf16[128,1536]{1,0:T(8,128)(2,1)S(1)} %collective-permute-done.6.refs_6_) | copy-start | bytes 1179652
  59.3 9.2 %collective-permute-start.16 = (bf16[2,16,16,128]{3,2,1,0:T(8,128)(2,1)S(1)}, bf16[2,16,16,128]{3,2,1,0:T(8,128)(2,1)S(1)}, u32[]{:S(2)}, u32[]{:S(2)}) collective-permute-start(bf16[2,16,16,128]{3,2,1,0:T(8,128)(2,1)S(1)} %bitcast.6), channel_id=1, source_target_pairs={{0,32},{16,48},{32,0},{48,16},{1,33},{17,49},{33,1},{49,17},{2,34}... | collective-permute-start | bytes 393224 | tf_op jit(solution)/shard_map/ppermute | solution.py:235
  61.7 13.0 %copy-start.9 = (bf16[128,1536]{1,0:T(8,128)(2,1)}, bf16[128,1536]{1,0:T(8,128)(2,1)S(1)}, u32[]{:S(2)}) copy-start(bf16[128,1536]{1,0:T(8,128)(2,1)S(1)} %collective-permute-done.7.refs_7_) | copy-start | bytes 1179652
  61.7 8.8 %collective-permute-start.17 = (bf16[2,16,16,128]{3,2,1,0:T(8,128)(2,1)S(1)}, bf16[2,16,16,128]{3,2,1,0:T(8,128)(2,1)S(1)}, u32[]{:S(2)}, u32[]{:S(2)}) collective-permute-start(bf16[2,16,16,128]{3,2,1,0:T(8,128)(2,1)S(1)} %bitcast.7), channel_id=1, source_target_pairs={{0,48},{16,0},{32,16},{48,32},{1,49},{17,1},{33,17},{49,33},{2,50}... | collective-permute-start | bytes 393224 | tf_op jit(solution)/shard_map/ppermute | solution.py:235
  62.9 16.5 %collective-permute-start.2 = (bf16[128,1536]{1,0:T(8,128)(2,1)}, bf16[128,1536]{1,0:T(8,128)(2,1)S(1)}, u32[]{:S(2)}, u32[]{:S(2)}) collective-permute-start(bf16[128,1536]{1,0:T(8,128)(2,1)} %get-tuple-element.90), channel_id=1, source_target_pairs={{0,14},{1,15},{2,8},{3,9},{4,10},{5,11},{6,12},{7,13},{8,6},{9,7},... | collective-permute-start | bytes 1179656 | tf_op jit(solution)/shard_map/ppermute | solution.py:244
  66.3 13.1 %collective-permute-start.3 = (bf16[128,1536]{1,0:T(8,128)(2,1)}, bf16[128,1536]{1,0:T(8,128)(2,1)S(1)}, u32[]{:S(2)}, u32[]{:S(2)}) collective-permute-start(bf16[128,1536]{1,0:T(8,128)(2,1)} %get-tuple-element.91), channel_id=1, source_target_pairs={{0,2},{1,3},{2,4},{3,5},{4,6},{5,7},{6,0},{7,1},{8,10},{9,11},{10,... | collective-permute-start | bytes 1179656 | tf_op jit(solution)/shard_map/ppermute | solution.py:244
  66.3 18.6 %collective-permute-start.8 = (bf16[128,1536]{1,0:T(8,128)(2,1)}, bf16[128,1536]{1,0:T(8,128)(2,1)S(1)}, u32[]{:S(2)}, u32[]{:S(2)}) collective-permute-start(bf16[128,1536]{1,0:T(8,128)(2,1)} %get-tuple-element.100), channel_id=1, source_target_pairs={{0,12},{1,13},{2,14},{3,15},{4,8},{5,9},{6,10},{7,11},{8,4},{9,5},... | collective-permute-start | bytes 1179656 | tf_op jit(solution)/shard_map/ppermute | solution.py:244
  68.5 16.4 %collective-permute-start.9 = (bf16[128,1536]{1,0:T(8,128)(2,1)}, bf16[128,1536]{1,0:T(8,128)(2,1)S(1)}, u32[]{:S(2)}, u32[]{:S(2)}) collective-permute-start(bf16[128,1536]{1,0:T(8,128)(2,1)} %get-tuple-element.101), channel_id=1, source_target_pairs={{0,1},{1,0},{2,3},{3,2},{4,5},{5,4},{6,7},{7,6},{8,9},{9,8},{10,11... | collective-permute-start | bytes 1179656 | tf_op jit(solution)/shard_map/ppermute | solution.py:244
  70.5 24.5 %collective-permute-start.14 = (bf16[128,1536]{1,0:T(8,128)(2,1)}, bf16[128,1536]{1,0:T(8,128)(2,1)S(1)}, u32[]{:S(2)}, u32[]{:S(2)}) collective-permute-start(bf16[128,1536]{1,0:T(8,128)(2,1)} %get-tuple-element.110), channel_id=1, source_target_pairs={{0,13},{1,12},{2,15},{3,14},{4,9},{5,8},{6,11},{7,10},{8,5},{9,4},... | collective-permute-start | bytes 1179656 | tf_op jit(solution)/shard_map/ppermute | solution.py:244

commit v3 on v2

--- a/solution.py
+++ b/solution.py
@@ -17,10 +17,10 @@
 ROUNDS = (
     ((1, 0, 1), (0, 2, 1)),
     ((1, 0, 0), (0, 2, 0)),
+    ((1, 1, 0), (0, 3, 0)),
     ((1, 1, 1), (0, 3, 1)),
-    ((1, 1, 0), (0, 3, 0)),
+    ((1, 3, 0), (0, 1, 0)),
     ((1, 3, 1), (0, 1, 1)),
-    ((1, 3, 0), (0, 1, 0)),
     ((1, 2, 0), (0, 0, 1)),
     ((1, 2, 1), (0, 0, 0)),
 )
@@ -28,10 +28,11 @@
 FINALS = (
     (((0, 0), (0, 1), (1, 0), (1, 1), (2, 0), (2, 1), (3, 0), (3, 1), (7, 1)), False),
     (((4, 0), (4, 1)), True),
-    (((5, 0), (5, 1), (6, 0), (6, 1), (7, 0)), True),
+    (((5, 0), (5, 1), (6, 0), (6, 1)), True),
+    (((7, 0),), True),
 )
 DEPTH = 3
-NEAR = (0, 1, 2)
+NEAR = (0, 1, 2, 3)
 ANY = pl.BlockSpec(memory_space=pltpu.HBM)
 VMEM = pl.BlockSpec(memory_space=pltpu.VMEM)
 

time: 96.6 us -> 97.8 us (1.012)
  starting transfers between devices: 38 us -> 39 us
    pallas_call x4, Pallas kernels: 11.5 us -> 10.3 us  [merge_chunks(): pl.pallas_call(body, in_specs=[ANY] * 4 + [VMEM] * len(old), out_specs=[V...]
    ppermute x15, starting transfers between devices: 33.1 us -> 34.1 us  [shards(): moved.append(lax.ppermute(v, SHARD, ring(s)) if any(s) else v)]
    pallas_call x3 -> x4, Pallas kernels: 6.03 us -> 6.72 us  [finish(): pl.pallas_call(body, in_specs=[pl.BlockSpec(memory_space=space)] * n + [V...]
  transfers between devices with their start and end apart: 18 -> 18, of which waited for: 5 -> 4; matrix products, arithmetic and copies ran while one was open for 0% -> 0% of each run, Pallas kernels for 16% -> 16%
where the time goes in v3:
time: 97.8 us; the launch traced here: 97.6 us
  starting transfers between devices  39 us (40%)
  waiting for transfers between devices  24 us (25%)
  Pallas kernels  18.3 us (19%)
  blocking collectives  15.5 us (16%)
    ppermute x15, starting transfers between devices, shards(): moved.append(lax.ppermute(v, SHARD, ring(s)) if any(s) else v)  34.1 us
    ppermute x15, waiting for transfers between devices, shards(): moved.append(lax.ppermute(v, SHARD, ring(s)) if any(s) else v)  24 us
    all_to_all x1, blocking collectives, exchange(): return lax.all_to_all(x, axes, 0, 0, tiled=True)  15.5 us
    pallas_call x4, Pallas kernels, merge_chunks(): pl.pallas_call(body, in_specs=[ANY] * 4 + [VMEM] * len(old), out_specs=[V...  10.3 us
    pallas_call x4, Pallas kernels, finish(): pl.pallas_call(body, in_specs=[pl.BlockSpec(memory_space=space)] * n + [V...  6.72 us
    ppermute x3, starting transfers between devices, shards(): groups.append(lax.ppermute(cols, 'x', [(i, (i + d) % m) for i in range(m)]))  4.88 us
  transfers between devices with their start and end apart: 18, of which 4 were waited for; matrix products, arithmetic and copies ran while one was open for 0% of the time, Pallas kernels for 16%

profile of v3, /device:TPU:1, one launch (start us, length us, event | category | flops | bytes accessed | tf_op | source)
XLA Modules:
  0.0 97.6 jit_solution(16743807379702547995)
XLA Ops:
  0.6 1.8 %merge.4 = (bf16[128,1536]{1,0:T(8,128)(2,1)S(1)}, bf16[128,1536]{1,0:T(8,128)(2,1)S(1)}, f32[2,12,128]{2,1,0:T(8,128)S(1)}) custom-call(f32[16,128,768]{2,1,0:T(8,128)} %refs_0_.4, bf16[16,128,768]{2,1,0:T(8,128)(2,1)} %refs_1_.4, f32[16,128,768]{2,1,0:T(8,128)} %refs_2_.4, bf16[16,128,768]{2,1,0:T(8,128)(2,1)} %refs_3_.4), custom_call_target="tpu_custom_call" | custom-call | tf_op jit(solution)/shard_map/merge/pallas_call | solution.py:119
  2.4 5.1 %collective-permute-start.9 = (bf16[128,1536]{1,0:T(8,128)(2,1)S(1)}, bf16[128,1536]{1,0:T(8,128)(2,1)S(1)}, u32[]{:S(2)}, u32[]{:S(2)}) collective-permute-start(bf16[128,1536]{1,0:T(8,128)(2,1)S(1)} %get-tuple-element.108), channel_id=1, source_target_pairs={{0,9},{1,8},{2,11},{3,10},{4,13},{5,12},{6,15},{7,14},{8,1},{9,0},... | collective-permute-start | bytes 1179656 | tf_op jit(solution)/shard_map/ppermute | solution.py:245
  7.5 2.6 %collective-permute-start.10 = (bf16[128,1536]{1,0:T(8,128)(2,1)S(1)}, bf16[128,1536]{1,0:T(8,128)(2,1)S(1)}, u32[]{:S(2)}, u32[]{:S(2)}) collective-permute-start(bf16[128,1536]{1,0:T(8,128)(2,1)S(1)} %get-tuple-element.109), channel_id=1, source_target_pairs={{0,5},{1,4},{2,7},{3,6},{4,1},{5,0},{6,3},{7,2},{8,13},{9,12},{10,... | collective-permute-start | bytes 1179656 | tf_op jit(solution)/shard_map/ppermute | solution.py:245
  10.1 2.6 %merge.5 = (bf16[128,1536]{1,0:T(8,128)(2,1)S(1)}, bf16[128,1536]{1,0:T(8,128)(2,1)S(1)}, bf16[128,1536]{1,0:T(8,128)(2,1)S(1)}, bf16[128,1536]{1,0:T(8,128)(2,1)S(1)}, f32[4,12,128]{2,1,0:T(8,128)S(1)}) custom-call(f32[16,128,768]{2,1,0:T(8,128)} %refs_0_.4, bf16[16,128,768]{2,1,0:T(8,128)(2,1)} %refs_1_.4, f32[16,128,768]{2,1,0:T(8,128)} %refs_2_.4, ...), custom_call_target="tpu_custom_call" | custom-call | tf_op jit(solution)/shard_map/merge/pallas_call | solution.py:119
  12.7 0.5 collective-permute-start
  13.1 0.1 collective-permute-start.1
  13.2 3.6 %collective-permute-start.5 = (bf16[128,1536]{1,0:T(8,128)(2,1)S(1)}, bf16[128,1536]{1,0:T(8,128)(2,1)S(1)}, u32[]{:S(2)}, u32[]{:S(2)}) collective-permute-start(bf16[128,1536]{1,0:T(8,128)(2,1)S(1)} %get-tuple-element.100), channel_id=1, source_target_pairs={{0,10},{1,11},{2,12},{3,13},{4,14},{5,15},{6,8},{7,9},{8,2},{9,3},... | collective-permute-start | bytes 1179656 | tf_op jit(solution)/shard_map/ppermute | solution.py:245
  16.8 2.6 %merge.6 = (bf16[128,1536]{1,0:T(8,128)(2,1)S(1)}, bf16[128,1536]{1,0:T(8,128)(2,1)S(1)}, bf16[128,1536]{1,0:T(8,128)(2,1)S(1)}, bf16[128,1536]{1,0:T(8,128)(2,1)S(1)}, f32[4,12,128]{2,1,0:T(8,128)S(1)}) custom-call(f32[16,128,768]{2,1,0:T(8,128)} %refs_0_.4, bf16[16,128,768]{2,1,0:T(8,128)(2,1)} %refs_1_.4, f32[16,128,768]{2,1,0:T(8,128)} %refs_2_.4, ...), custom_call_target="tpu_custom_call" | custom-call | tf_op jit(solution)/shard_map/merge/pallas_call | solution.py:119
  19.4 0.0 collective-permute-done.9.refs_0_
  19.4 1.7 %collective-permute-start.6 = (bf16[128,1536]{1,0:T(8,128)(2,1)S(1)}, bf16[128,1536]{1,0:T(8,128)(2,1)S(1)}, u32[]{:S(2)}, u32[]{:S(2)}) collective-permute-start(bf16[128,1536]{1,0:T(8,128)(2,1)S(1)} %get-tuple-element.101), channel_id=1, source_target_pairs={{0,6},{1,7},{2,0},{3,1},{4,2},{5,3},{6,4},{7,5},{8,14},{9,15},{10,... | collective-permute-start | bytes 1179656 | tf_op jit(solution)/shard_map/ppermute | solution.py:245
  21.1 0.0 collective-permute-done.10.refs_1_
  21.1 1.1 %collective-permute-start.11 = (bf16[128,1536]{1,0:T(8,128)(2,1)S(1)}, bf16[128,1536]{1,0:T(8,128)(2,1)S(1)}, u32[]{:S(2)}, u32[]{:S(2)}) collective-permute-start(bf16[128,1536]{1,0:T(8,128)(2,1)S(1)} %get-tuple-element.110), channel_id=1, source_target_pairs={{0,11},{1,10},{2,13},{3,12},{4,15},{5,14},{6,9},{7,8},{8,3},{9,2},... | collective-permute-start | bytes 1179656 | tf_op jit(solution)/shard_map/ppermute | solution.py:245
  22.1 2.8 %collective-permute-done.refs_2_ = bf16[128,1536]{1,0:T(8,128)(2,1)S(1)} collective-permute-done((bf16[128,1536]{1,0:T(8,128)(2,1)S(1)}, bf16[128,1536]{1,0:T(8,128)(2,1)S(1)}, u32[]{:S(2)}, u32[]{:S(2)}) %collective-permute-start) | collective-permute-done | bytes 393248 | tf_op jit(solution)/shard_map/ppermute | solution.py:245
  24.9 3.3 %collective-permute-start.12 = (bf16[128,1536]{1,0:T(8,128)(2,1)S(1)}, bf16[128,1536]{1,0:T(8,128)(2,1)S(1)}, u32[]{:S(2)}, u32[]{:S(2)}) collective-permute-start(bf16[128,1536]{1,0:T(8,128)(2,1)S(1)} %get-tuple-element.111), channel_id=1, source_target_pairs={{0,7},{1,6},{2,1},{3,0},{4,3},{5,2},{6,5},{7,4},{8,15},{9,14},{10,... | collective-permute-start | bytes 1179656 | tf_op jit(solution)/shard_map/ppermute | solution.py:245
  28.2 0.0 collective-permute-done.1.refs_3_
  28.2 3.6 %collective-permute-start.2 = (bf16[128,1536]{1,0:T(8,128)(2,1)S(1)}, bf16[128,1536]{1,0:T(8,128)(2,1)S(1)}, u32[]{:S(2)}, u32[]{:S(2)}) collective-permute-start(bf16[128,1536]{1,0:T(8,128)(2,1)S(1)} %get-tuple-element.94), channel_id=1, source_target_pairs={{0,14},{1,15},{2,8},{3,9},{4,10},{5,11},{6,12},{7,13},{8,6},{9,7},... | collective-permute-start | bytes 1179656 | tf_op jit(solution)/shard_map/ppermute | solution.py:245
  31.8 4.8 %collective-permute-done.5.refs_4_ = bf16[128,1536]{1,0:T(8,128)(2,1)S(1)} collective-permute-done((bf16[128,1536]{1,0:T(8,128)(2,1)S(1)}, bf16[128,1536]{1,0:T(8,128)(2,1)S(1)}, u32[]{:S(2)}, u32[]{:S(2)}) %collective-permute-start.5) | collective-permute-done | bytes 393248 | tf_op jit(solution)/shard_map/ppermute | solution.py:245
  36.7 1.5 %collective-permute-start.3 = (bf16[128,1536]{1,0:T(8,128)(2,1)S(1)}, bf16[128,1536]{1,0:T(8,128)(2,1)S(1)}, u32[]{:S(2)}, u32[]{:S(2)}) collective-permute-start(bf16[128,1536]{1,0:T(8,128)(2,1)S(1)} %get-tuple-element.95), channel_id=1, source_target_pairs={{0,2},{1,3},{2,4},{3,5},{4,6},{5,7},{6,0},{7,1},{8,10},{9,11},{10,... | collective-permute-start | bytes 1179656 | tf_op jit(solution)/shard_map/ppermute | solution.py:245
  38.2 0.0 copy-done.2
  38.2 3.4 %merge.7 = (bf16[128,1536]{1,0:T(8,128)(2,1)S(1)}, bf16[128,1536]{1,0:T(8,128)(2,1)S(1)}, bf16[128,1536]{1,0:T(8,128)(2,1)S(1)}, bf16[128,1536]{1,0:T(8,128)(2,1...) custom-call(f32[16,128,768]{2,1,0:T(8,128)} %refs_0_.4, ...), custom_call_target="tpu_custom_call" | custom-call | tf_op jit(solution)/shard_map/merge/pallas_call | solution.py:119
  41.7 15.5 %all_to_all.5.refs_9_.refs_2_.refs_4_.refs_1_ = bf16[32,32,128]{2,1,0:T(8,128)(2,1)S(1)} all-to-all(bf16[32,32,128]{2,1,0:T(8,128)(2,1)S(1)} %get-tuple-element.97), channel_id=1, replica_groups=mesh['zl'=2,'x'=4,'zh'=2,'y'=4,'c'=2] {'zl','zh','y','c'}, dimensions={0} | all-to-all | bytes 524288 | tf_op jit(solution)/shard_map/all_to_all | solution.py:210
  57.2 0.0 collective-permute-done.6.refs_5_
  57.2 1.3 %collective-permute-start.15 = (bf16[2,16,16,128]{3,2,1,0:T(8,128)(2,1)S(1)}, bf16[2,16,16,128]{3,2,1,0:T(8,128)(2,1)S(1)}, u32[]{:S(2)}, u32[]{:S(2)}) collective-permute-start(bf16[2,16,16,128]{3,2,1,0:T(8,128)(2,1)S(1)} %bitcast.5), channel_id=1, source_target_pairs={{0,16},{16,32},{32,48},{48,0},{1,17},{17,33},{33,49},{49,1},{2,18}... | collective-permute-start | bytes 393224 | tf_op jit(solution)/shard_map/ppermute | solution.py:236
  58.5 0.0 collective-permute-done.11.refs_6_
  58.5 2.5 %collective-permute-start.16 = (bf16[2,16,16,128]{3,2,1,0:T(8,128)(2,1)S(1)}, bf16[2,16,16,128]{3,2,1,0:T(8,128)(2,1)S(1)}, u32[]{:S(2)}, u32[]{:S(2)}) collective-permute-start(bf16[2,16,16,128]{3,2,1,0:T(8,128)(2,1)S(1)} %bitcast.6), channel_id=1, source_target_pairs={{0,32},{16,48},{32,0},{48,16},{1,33},{17,49},{33,1},{49,17},{2,34}... | collective-permute-start | bytes 393224 | tf_op jit(solution)/shard_map/ppermute | solution.py:236
  61.0 0.0 collective-permute-done.12.refs_7_
  61.0 1.2 %collective-permute-start.17 = (bf16[2,16,16,128]{3,2,1,0:T(8,128)(2,1)S(1)}, bf16[2,16,16,128]{3,2,1,0:T(8,128)(2,1)S(1)}, u32[]{:S(2)}, u32[]{:S(2)}) collective-permute-start(bf16[2,16,16,128]{3,2,1,0:T(8,128)(2,1)S(1)} %bitcast.7), channel_id=1, source_target_pairs={{0,48},{16,0},{32,16},{48,32},{1,49},{17,1},{33,17},{49,33},{2,50}... | collective-permute-start | bytes 393224 | tf_op jit(solution)/shard_map/ppermute | solution.py:236
  62.1 0.0 collective-permute-done.2.refs_0_
  62.1 5.3 %collective-permute-start.7 = (bf16[128,1536]{1,0:T(8,128)(2,1)S(1)}, bf16[128,1536]{1,0:T(8,128)(2,1)S(1)}, u32[]{:S(2)}, u32[]{:S(2)}) collective-permute-start(bf16[128,1536]{1,0:T(8,128)(2,1)S(1)} %get-tuple-element.102), channel_id=1, source_target_pairs={{0,15},{1,14},{2,9},{3,8},{4,11},{5,10},{6,13},{7,12},{8,7},{9,6},... | collective-permute-start | bytes 1179656 | tf_op jit(solution)/shard_map/ppermute | solution.py:245
  67.4 0.0 collective-permute-done.3.refs_1_
  67.4 0.0 collective-permute-start.8
  67.4 0.0 collective-permute-done.15.refs_1_
  67.4 1.5 %collective-permute-start.13 = (bf16[128,1536]{1,0:T(8,128)(2,1)S(1)}, bf16[128,1536]{1,0:T(8,128)(2,1)S(1)}, u32[]{:S(2)}, u32[]{:S(2)}) collective-permute-start(bf16[128,1536]{1,0:T(8,128)(2,1)S(1)} %get-tuple-element.112), channel_id=1, source_target_pairs={{0,12},{1,13},{2,14},{3,15},{4,8},{5,9},{6,10},{7,11},{8,4},{9,5},... | collective-permute-start | bytes 1179656 | tf_op jit(solution)/shard_map/ppermute | solution.py:245
  68.9 0.0 copy-done
  68.9 0.0 collective-permute-done.16.refs_2_
  68.9 1.5 %collective-permute-start.14 = (bf16[128,1536]{1,0:T(8,128)(2,1)S(1)}, bf16[128,1536]{1,0:T(8,128)(2,1)S(1)}, u32[]{:S(2)}, u32[]{:S(2)}) collective-permute-start(bf16[128,1536]{1,0:T(8,128)(2,1)S(1)} %get-tuple-element.113), channel_id=1, source_target_pairs={{0,1},{1,0},{2,3},{3,2},{4,5},{5,4},{6,7},{7,6},{8,9},{9,8},{10,11... | collective-permute-start | bytes 1179656 | tf_op jit(solution)/shard_map/ppermute | solution.py:245
  70.4 0.0 collective-permute-done.17.refs_3_
  70.4 2.9 %collective-permute-start.4 = (bf16[128,1536]{1,0:T(8,128)(2,1)S(1)}, bf16[128,1536]{1,0:T(8,128)(2,1)S(1)}, u32[]{:S(2)}, u32[]{:S(2)}) collective-permute-start(bf16[128,1536]{1,0:T(8,128)(2,1)S(1)} %get-tuple-element.96), channel_id=1, source_target_pairs={{0,13},{1,12},{2,15},{3,14},{4,9},{5,8},{6,11},{7,10},{8,5},{9,4},... | collective-permute-start | bytes 1179656 | tf_op jit(solution)/shard_map/ppermute | solution.py:245
  73.3 1.2 %lay_router.1 = bf16[2048,128]{1,0:T(8,128)(2,1)} custom-call(bf16[2,16,16,128]{3,2,1,0:T(8,128)(2,1)S(1)} %bitcast.8, bf16[2,16,16,128]{3,2,1,0:T(8,128)(2,1)S(1)} %collective-permute-done.15.refs_1_, bf16[2,16,16,128]{3,2,1,0:T(8,128)(2,1)S(1)} %collective-permute-done.16.refs_2_, bf16[2,16,16,128]{3,2,1,0:T(8,128)(2,1)S(1)} %collective-permute-done.17.refs_3_), custom_call_target="tpu_custom_call" | custom-call | tf_op jit(solution)/shard_map/lay_router/pallas_call | solution.py:200
  74.5 3.6 %finish.4 = (bf16[2048,768]{1,0:T(8,128)(2,1)}, bf16[2048,768]{1,0:T(8,128)(2,1)}, f32[1,768]{1,0:T(1,128)}, f32[1,768]{1,0:T(1,128)}) custom-call(bf16[128,1536]{1,0:T(8,128)(2,1)} %copy-done.3, bf16[128,1536]{1,0:T(8,128)(2,1)} %copy-done.4, bf16[128,1536]{1,0:T(8,128)(2,1)} %copy-done.5, bf16[128,1536]{1,0:T(8,128)(2,1)} %copy-done.6, ...), custom_call_target="tpu_custom_call" | custom-call | tf_op jit(solution)/shard_map/finish/pallas_call | solution.py:173
  78.1 1.0 %finish.5 = (bf16[2048,768]{1,0:T(8,128)(2,1)}, bf16[2048,768]{1,0:T(8,128)(2,1)}) custom-call(bf16[128,1536]{1,0:T(8,128)(2,1)S(1)} %collective-permute-done.2.refs_0_, bf16[128,1536]{1,0:T(8,128)(2,1)S(1)} %collective-permute-done.3.refs_1_, ...), custom_call_target="tpu_custom_call", output_to_operand_aliasing={{0}: (3, {}), {1}: (4, {})} | custom-call | tf_op jit(solution)/shard_map/finish/pallas_call | solution.py:173
  79.1 13.5 %collective-permute-done.7.refs_0_ = bf16[128,1536]{1,0:T(8,128)(2,1)S(1)} collective-permute-done((bf16[128,1536]{1,0:T(8,128)(2,1)S(1)}, bf16[128,1536]{1,0:T(8,128)(2,1)S(1)}, u32[]{:S(2)}, u32[]{:S(2)}) %collective-permute-start.7) | collective-permute-done | bytes 393248 | tf_op jit(solution)/shard_map/ppermute | solution.py:245
  92.6 2.8 %collective-permute-done.8.refs_1_ = bf16[128,1536]{1,0:T(8,128)(2,1)S(1)} collective-permute-done((bf16[128,1536]{1,0:T(8,128)(2,1)S(1)}, bf16[128,1536]{1,0:T(8,128)(2,1)S(1)}, u32[]{:S(2)}, u32[]{:S(2)}) %collective-permute-start.8) | collective-permute-done | bytes 393248 | tf_op jit(solution)/shard_map/ppermute | solution.py:245
  95.5 0.0 collective-permute-done.13.refs_2_
  95.5 0.0 collective-permute-done.14.refs_3_
  95.5 1.3 %finish.6 = (bf16[2048,768]{1,0:T(8,128)(2,1)}, bf16[2048,768]{1,0:T(8,128)(2,1)}) custom-call(bf16[128,1536]{1,0:T(8,128)(2,1)S(1)} %collective-permute-done.7.refs_0_, bf16[128,1536]{1,0:T(8,128)(2,1)S(1)} %collective-permute-done.8.refs_1_, bf16[128,1536]{1,0:T(8,128)(2,1)S(1)} %collective-permute-done.13.refs_2_, ...), custom_call_target="tpu_custom_call", output_to_operand_aliasing={{0}: (5, {}), {1}: (6, {})} | custom-call | tf_op jit(solution)/shard_map/finish/pallas_call | solution.py:173
  96.8 0.0 collective-permute-done.4.refs_0_
  96.8 0.8 finish.7
  (21 shorter events, 0.0 us)
Async XLA Ops:
  2.4 17.0 %collective-permute-start.9 = (bf16[128,1536]{1,0:T(8,128)(2,1)S(1)}, bf16[128,1536]{1,0:T(8,128)(2,1)S(1)}, u32[]{:S(2)}, u32[]{:S(2)}) collective-permute-start(bf16[128,1536]{1,0:T(8,128)(2,1)S(1)} %get-tuple-element.108), channel_id=1, source_target_pairs={{0,9},{1,8},{2,11},{3,10},{4,13},{5,12},{6,15},{7,14},{8,1},{9,0},... | collective-permute-start | bytes 1179656 | tf_op jit(solution)/shard_map/ppermute | solution.py:245
  7.5 13.6 %collective-permute-start.10 = (bf16[128,1536]{1,0:T(8,128)(2,1)S(1)}, bf16[128,1536]{1,0:T(8,128)(2,1)S(1)}, u32[]{:S(2)}, u32[]{:S(2)}) collective-permute-start(bf16[128,1536]{1,0:T(8,128)(2,1)S(1)} %get-tuple-element.109), channel_id=1, source_target_pairs={{0,5},{1,4},{2,7},{3,6},{4,1},{5,0},{6,3},{7,2},{8,13},{9,12},{10,... | collective-permute-start | bytes 1179656 | tf_op jit(solution)/shard_map/ppermute | solution.py:245
  12.7 12.2 %collective-permute-start = (bf16[128,1536]{1,0:T(8,128)(2,1)S(1)}, bf16[128,1536]{1,0:T(8,128)(2,1)S(1)}, u32[]{:S(2)}, u32[]{:S(2)}) collective-permute-start(bf16[128,1536]{1,0:T(8,128)(2,1)S(1)} %get-tuple-element.92), channel_id=1, source_target_pairs={{0,8},{1,9},{2,10},{3,11},{4,12},{5,13},{6,14},{7,15},{8,0},{9,1},... | collective-permute-start | bytes 1179656 | tf_op jit(solution)/shard_map/ppermute | solution.py:245
  13.1 15.1 %collective-permute-start.1 = (bf16[128,1536]{1,0:T(8,128)(2,1)S(1)}, bf16[128,1536]{1,0:T(8,128)(2,1)S(1)}, u32[]{:S(2)}, u32[]{:S(2)}) collective-permute-start(bf16[128,1536]{1,0:T(8,128)(2,1)S(1)} %get-tuple-element.93), channel_id=1, source_target_pairs={{0,4},{1,5},{2,6},{3,7},{4,0},{5,1},{6,2},{7,3},{8,12},{9,13},{10,... | collective-permute-start | bytes 1179656 | tf_op jit(solution)/shard_map/ppermute | solution.py:245
  13.2 25.0 %copy-start.1 = (f32[128,16]{0,1:T(8,128)S(1)}, f32[128,16]{0,1:T(8,128)}, u32[]{:S(2)}) copy-start(f32[128,16]{0,1:T(8,128)} %param.10) | copy-start | bytes 24580
  13.2 25.0 %copy-start.2 = (f32[128]{0:T(128)S(1)}, f32[128]{0:T(128)}, u32[]{:S(2)}) copy-start(f32[128]{0:T(128)} %param.11) | copy-start | bytes 1540
  13.2 23.5 %collective-permute-start.5 = (bf16[128,1536]{1,0:T(8,128)(2,1)S(1)}, bf16[128,1536]{1,0:T(8,128)(2,1)S(1)}, u32[]{:S(2)}, u32[]{:S(2)}) collective-permute-start(bf16[128,1536]{1,0:T(8,128)(2,1)S(1)} %get-tuple-element.100), channel_id=1, source_target_pairs={{0,10},{1,11},{2,12},{3,13},{4,14},{5,15},{6,8},{7,9},{8,2},{9,3},... | collective-permute-start | bytes 1179656 | tf_op jit(solution)/shard_map/ppermute | solution.py:245
  19.4 22.3 %copy-start.3 = (bf16[128,1536]{1,0:T(8,128)(2,1)}, bf16[128,1536]{1,0:T(8,128)(2,1)S(1)}, u32[]{:S(2)}) copy-start(bf16[128,1536]{1,0:T(8,128)(2,1)S(1)} %collective-permute-done.9.refs_0_) | copy-start | bytes 1179652
  19.4 37.8 %collective-permute-start.6 = (bf16[128,1536]{1,0:T(8,128)(2,1)S(1)}, bf16[128,1536]{1,0:T(8,128)(2,1)S(1)}, u32[]{:S(2)}, u32[]{:S(2)}) collective-permute-start(bf16[128,1536]{1,0:T(8,128)(2,1)S(1)} %get-tuple-element.101), channel_id=1, source_target_pairs={{0,6},{1,7},{2,0},{3,1},{4,2},{5,3},{6,4},{7,5},{8,14},{9,15},{10,... | collective-permute-start | bytes 1179656 | tf_op jit(solution)/shard_map/ppermute | solution.py:245
  21.1 20.6 %copy-start.4 = (bf16[128,1536]{1,0:T(8,128)(2,1)}, bf16[128,1536]{1,0:T(8,128)(2,1)S(1)}, u32[]{:S(2)}) copy-start(bf16[128,1536]{1,0:T(8,128)(2,1)S(1)} %collective-permute-done.10.refs_1_) | copy-start | bytes 1179652
  21.1 37.4 %collective-permute-start.11 = (bf16[128,1536]{1,0:T(8,128)(2,1)S(1)}, bf16[128,1536]{1,0:T(8,128)(2,1)S(1)}, u32[]{:S(2)}, u32[]{:S(2)}) collective-permute-start(bf16[128,1536]{1,0:T(8,128)(2,1)S(1)} %get-tuple-element.110), channel_id=1, source_target_pairs={{0,11},{1,10},{2,13},{3,12},{4,15},{5,14},{6,9},{7,8},{8,3},{9,2},... | collective-permute-start | bytes 1179656 | tf_op jit(solution)/shard_map/ppermute | solution.py:245
  24.9 16.7 %copy-start.5 = (bf16[128,1536]{1,0:T(8,128)(2,1)}, bf16[128,1536]{1,0:T(8,128)(2,1)S(1)}, u32[]{:S(2)}) copy-start(bf16[128,1536]{1,0:T(8,128)(2,1)S(1)} %collective-permute-done.refs_2_) | copy-start | bytes 1179652
  24.9 36.0 %collective-permute-start.12 = (bf16[128,1536]{1,0:T(8,128)(2,1)S(1)}, bf16[128,1536]{1,0:T(8,128)(2,1)S(1)}, u32[]{:S(2)}, u32[]{:S(2)}) collective-permute-start(bf16[128,1536]{1,0:T(8,128)(2,1)S(1)} %get-tuple-element.111), channel_id=1, source_target_pairs={{0,7},{1,6},{2,1},{3,0},{4,3},{5,2},{6,5},{7,4},{8,15},{9,14},{10,... | collective-permute-start | bytes 1179656 | tf_op jit(solution)/shard_map/ppermute | solution.py:245
  28.2 13.4 %copy-start.6 = (bf16[128,1536]{1,0:T(8,128)(2,1)}, bf16[128,1536]{1,0:T(8,128)(2,1)S(1)}, u32[]{:S(2)}) copy-start(bf16[128,1536]{1,0:T(8,128)(2,1)S(1)} %collective-permute-done.1.refs_3_) | copy-start | bytes 1179652
  28.2 33.9 %collective-permute-start.2 = (bf16[128,1536]{1,0:T(8,128)(2,1)S(1)}, bf16[128,1536]{1,0:T(8,128)(2,1)S(1)}, u32[]{:S(2)}, u32[]{:S(2)}) collective-permute-start(bf16[128,1536]{1,0:T(8,128)(2,1)S(1)} %get-tuple-element.94), channel_id=1, source_target_pairs={{0,14},{1,15},{2,8},{3,9},{4,10},{5,11},{6,12},{7,13},{8,6},{9,7},... | collective-permute-start | bytes 1179656 | tf_op jit(solution)/shard_map/ppermute | solution.py:245
  36.7 5.0 %copy-start.7 = (bf16[128,1536]{1,0:T(8,128)(2,1)}, bf16[128,1536]{1,0:T(8,128)(2,1)S(1)}, u32[]{:S(2)}) copy-start(bf16[128,1536]{1,0:T(8,128)(2,1)S(1)} %collective-permute-done.5.refs_4_) | copy-start | bytes 1179652
  36.7 30.7 %collective-permute-start.3 = (bf16[128,1536]{1,0:T(8,128)(2,1)S(1)}, bf16[128,1536]{1,0:T(8,128)(2,1)S(1)}, u32[]{:S(2)}, u32[]{:S(2)}) collective-permute-start(bf16[128,1536]{1,0:T(8,128)(2,1)S(1)} %get-tuple-element.95), channel_id=1, source_target_pairs={{0,2},{1,3},{2,4},{3,5},{4,6},{5,7},{6,0},{7,1},{8,10},{9,11},{10,... | collective-permute-start | bytes 1179656 | tf_op jit(solution)/shard_map/ppermute | solution.py:245
  41.7 27.2 %copy-start = (bf16[128,1536]{1,0:T(8,128)(2,1)}, bf16[128,1536]{1,0:T(8,128)(2,1)S(1)}, u32[]{:S(2)}) copy-start(bf16[128,1536]{1,0:T(8,128)(2,1)S(1)} %get-tuple-element.124.refs_8_) | copy-start | bytes 1179652
  57.2 17.3 %copy-start.8 = (bf16[128,1536]{1,0:T(8,128)(2,1)}, bf16[128,1536]{1,0:T(8,128)(2,1)S(1)}, u32[]{:S(2)}) copy-start(bf16[128,1536]{1,0:T(8,128)(2,1)S(1)} %collective-permute-done.6.refs_5_) | copy-start | bytes 1179652
  57.2 10.2 %collective-permute-start.15 = (bf16[2,16,16,128]{3,2,1,0:T(8,128)(2,1)S(1)}, bf16[2,16,16,128]{3,2,1,0:T(8,128)(2,1)S(1)}, u32[]{:S(2)}, u32[]{:S(2)}) collective-permute-start(bf16[2,16,16,128]{3,2,1,0:T(8,128)(2,1)S(1)} %bitcast.5), channel_id=1, source_target_pairs={{0,16},{16,32},{32,48},{48,0},{1,17},{17,33},{33,49},{49,1},{2,18}... | collective-permute-start | bytes 393224 | tf_op jit(solution)/shard_map/ppermute | solution.py:236
  58.5 16.0 %copy-start.9 = (bf16[128,1536]{1,0:T(8,128)(2,1)}, bf16[128,1536]{1,0:T(8,128)(2,1)S(1)}, u32[]{:S(2)}) copy-start(bf16[128,1536]{1,0:T(8,128)(2,1)S(1)} %collective-permute-done.11.refs_6_) | copy-start | bytes 1179652
  58.5 10.4 %collective-permute-start.16 = (bf16[2,16,16,128]{3,2,1,0:T(8,128)(2,1)S(1)}, bf16[2,16,16,128]{3,2,1,0:T(8,128)(2,1)S(1)}, u32[]{:S(2)}, u32[]{:S(2)}) collective-permute-start(bf16[2,16,16,128]{3,2,1,0:T(8,128)(2,1)S(1)} %bitcast.6), channel_id=1, source_target_pairs={{0,32},{16,48},{32,0},{48,16},{1,33},{17,49},{33,1},{49,17},{2,34}... | collective-permute-start | bytes 393224 | tf_op jit(solution)/shard_map/ppermute | solution.py:236
  61.0 13.5 %copy-start.10 = (bf16[128,1536]{1,0:T(8,128)(2,1)}, bf16[128,1536]{1,0:T(8,128)(2,1)S(1)}, u32[]{:S(2)}) copy-start(bf16[128,1536]{1,0:T(8,128)(2,1)S(1)} %collective-permute-done.12.refs_7_) | copy-start | bytes 1179652
  61.0 9.5 %collective-permute-start.17 = (bf16[2,16,16,128]{3,2,1,0:T(8,128)(2,1)S(1)}, bf16[2,16,16,128]{3,2,1,0:T(8,128)(2,1)S(1)}, u32[]{:S(2)}, u32[]{:S(2)}) collective-permute-start(bf16[2,16,16,128]{3,2,1,0:T(8,128)(2,1)S(1)} %bitcast.7), channel_id=1, source_target_pairs={{0,48},{16,0},{32,16},{48,32},{1,49},{17,1},{33,17},{49,33},{2,50}... | collective-permute-start | bytes 393224 | tf_op jit(solution)/shard_map/ppermute | solution.py:236
  62.1 30.5 %collective-permute-start.7 = (bf16[128,1536]{1,0:T(8,128)(2,1)S(1)}, bf16[128,1536]{1,0:T(8,128)(2,1)S(1)}, u32[]{:S(2)}, u32[]{:S(2)}) collective-permute-start(bf16[128,1536]{1,0:T(8,128)(2,1)S(1)} %get-tuple-element.102), channel_id=1, source_target_pairs={{0,15},{1,14},{2,9},{3,8},{4,11},{5,10},{6,13},{7,12},{8,7},{9,6},... | collective-permute-start | bytes 1179656 | tf_op jit(solution)/shard_map/ppermute | solution.py:245
  67.4 28.1 %collective-permute-start.8 = (bf16[128,1536]{1,0:T(8,128)(2,1)S(1)}, bf16[128,1536]{1,0:T(8,128)(2,1)S(1)}, u32[]{:S(2)}, u32[]{:S(2)}) collective-permute-start(bf16[128,1536]{1,0:T(8,128)(2,1)S(1)} %get-tuple-element.103), channel_id=1, source_target_pairs={{0,3},{1,2},{2,5},{3,4},{4,7},{5,6},{6,1},{7,0},{8,11},{9,10},{10,... | collective-permute-start | bytes 1179656 | tf_op jit(solution)/shard_map/ppermute | solution.py:245
  67.4 28.1 %collective-permute-start.13 = (bf16[128,1536]{1,0:T(8,128)(2,1)S(1)}, bf16[128,1536]{1,0:T(8,128)(2,1)S(1)}, u32[]{:S(2)}, u32[]{:S(2)}) collective-permute-start(bf16[128,1536]{1,0:T(8,128)(2,1)S(1)} %get-tuple-element.112), channel_id=1, source_target_pairs={{0,12},{1,13},{2,14},{3,15},{4,8},{5,9},{6,10},{7,11},{8,4},{9,5},... | collective-permute-start | bytes 1179656 | tf_op jit(solution)/shard_map/ppermute | solution.py:245
  68.9 26.6 %collective-permute-start.14 = (bf16[128,1536]{1,0:T(8,128)(2,1)S(1)}, bf16[128,1536]{1,0:T(8,128)(2,1)S(1)}, u32[]{:S(2)}, u32[]{:S(2)}) collective-permute-start(bf16[128,1536]{1,0:T(8,128)(2,1)S(1)} %get-tuple-element.113), channel_id=1, source_target_pairs={{0,1},{1,0},{2,3},{3,2},{4,5},{5,4},{6,7},{7,6},{8,9},{9,8},{10,11... | collective-permute-start | bytes 1179656 | tf_op jit(solution)/shard_map/ppermute | solution.py:245
  70.4 26.4 %collective-permute-start.4 = (bf16[128,1536]{1,0:T(8,128)(2,1)S(1)}, bf16[128,1536]{1,0:T(8,128)(2,1)S(1)}, u32[]{:S(2)}, u32[]{:S(2)}) collective-permute-start(bf16[128,1536]{1,0:T(8,128)(2,1)S(1)} %get-tuple-element.96), channel_id=1, source_target_pairs={{0,13},{1,12},{2,15},{3,14},{4,9},{5,8},{6,11},{7,10},{8,5},{9,4},... | collective-permute-start | bytes 1179656 | tf_op jit(solution)/shard_map/ppermute | solution.py:245
